TPU v7x, 128 devices: a whole 4x4x4 slice. The times are simulated.
128 devices in a mesh: row: 16 (over x_hi, y, core), col: 4 (over z), dp: 2 (over x_lo).
Axes of the slice: x: 4 (x_hi: 2, x_lo: 2; x = x_hi * 2 + x_lo), y: 4, z: 4, core: 2. Of those that a mesh axis runs over, the one named last changes fastest.
Arguments:
- slides: bfloat16 [2, 256, 128, 512], P('dp', 'row', 'col'), may hold values from -6 to 6
- cotangent: bfloat16 [2, 256, 128, 512], P('dp', 'row', 'col'), may hold values from -6 to 6
- kernel: float32 [2, 7, 7, 512], replicated, may hold values from -0.875 to 0.875
- kernel_bias: float32 [2, 512], replicated, may hold values from -3 to 3
- norm_gain: float32 [2, 512], replicated, may hold values from 0.1 to 1.9
- norm_bias: float32 [2, 512], replicated, may hold values from -3 to 3
- weight_in: bfloat16 [2, 512, 2048], P(None, 'dp'), may hold values from -0.25 to 0.25
- bias_in: float32 [2, 2048], replicated, may hold values from -3 to 3
- weight_out: bfloat16 [2, 2048, 512], P(None, None, 'dp'), may hold values from -0.125 to 0.125
- bias_out: float32 [2, 512], replicated, may hold values from -3 to 3
- layer_scale: float32 [2, 512], replicated, may hold values from 0.3 to 1.5
Outputs:
- output: bfloat16 [2, 256, 128, 512], P('dp', 'row', 'col')
- grad_slides: bfloat16 [2, 256, 128, 512], P('dp', 'row', 'col')
- grad_weight_in: float32 [2, 512, 2048], P(None, 'dp')
- grad_weight_out: float32 [2, 2048, 512], P(None, None, 'dp')
- grad_kernel: float32 [2, 7, 7, 512], replicated
- grad_channel: float32 [2, 5, 512], replicated
- grad_bias_in: float32 [2, 2048], replicated
All inputs are finite; a program needn't handle non-finite values.
Results may differ from a plain program's by a relative error of at most 0.01.
Values may be sent and summed in bfloat16 or wider, within the bound.
A program may use at most 128 MiB of HBM per device.

v0:
```python
import jax
import jax.numpy as jnp
from jax import lax
from jax.sharding import PartitionSpec as P

COEF = 0.7978845608028654
CUBIC = 0.044715
EPSILON = 1e-06


def cut_along(shard, dim, size):
    before, after = (shard.shape[:dim], shard.shape[dim + 1 :])
    return jnp.moveaxis(shard.reshape(*before, size, -1, *after), dim, 0)


def sent_and_summed(shard, axis, dim):
    size = lax.axis_size(axis)
    pieces = lax.all_to_all(cut_along(shard, dim, size), axis, 0, 0, tiled=True)
    return jnp.sum(pieces.astype(jnp.float32), axis=0)


def padded_to(lines, size):
    spare = -len(lines) % size
    return jnp.pad(lines, [(0, spare)] + [(0, 0)] * (lines.ndim - 1))


def copy_for_each(shard, axis):
    copies = jnp.broadcast_to(shard, (lax.axis_size(axis), *shard.shape))
    return lax.all_to_all(copies, axis, split_axis=0, concat_axis=0, tiled=True)


def in_order(pieces, dim):
    pieces = jnp.moveaxis(pieces, 0, dim)
    lengths = pieces.shape
    return pieces.reshape(*lengths[:dim], lengths[dim] * lengths[dim + 1], *lengths[dim + 2 :])


def gather_directly(shard, axis, dim):
    pieces = copy_for_each(shard, axis)
    return in_order(pieces, dim)


def total_of(shard, axes):
    lines = shard.reshape(-1, shard.shape[-1])
    padded = padded_to(lines, lax.axis_size(axes))
    whole = gather_directly(sent_and_summed(padded, axes, 0).astype(jnp.bfloat16), axes, 0)
    return lax.slice_in_dim(whole, 0, len(lines)).reshape(shard.shape).astype(jnp.float32)


def turned_gather(arrays, axis, dims):
    turned = [jnp.moveaxis(a, dim, 0) for a, dim in zip(arrays, dims)]
    widths = [t[0].size for t in turned]
    both = jnp.concatenate([t.reshape(-1, w) for t, w in zip(turned, widths)], axis=1)
    result = lax.all_gather(both, axis, axis=0, tiled=True)
    pieces = jnp.split(result, [sum(widths[:k]) for k in range(1, len(widths))], axis=1)
    return tuple(
        (
            jnp.moveaxis(b.reshape(-1, *t.shape[1:]), 0, dim)
            for b, t, dim in zip(pieces, turned, dims)
        )
    )


def with_halo(block, sides, width):
    for axis, dim in sides:
        count = lax.axis_size(axis)
        forward = [(i, i + 1) for i in range(count - 1)]
        backward = [(target, source) for source, target in forward]
        low = lax.ppermute(
            lax.slice_in_dim(block, block.shape[dim] - width, None, axis=dim), axis, forward
        )
        high = lax.ppermute(lax.slice_in_dim(block, 0, width, axis=dim), axis, backward)
        block = jnp.concatenate([low, block, high], axis=dim)
    return block


def gelu_tanh(values):
    inner = COEF * (values + CUBIC * values * values * values)
    return 0.5 * values * (1.0 + jnp.tanh(inner))


def gelu_slope(values):
    tangent = jnp.tanh(COEF * (values + CUBIC * values * values * values))
    return 0.5 * (1.0 + tangent) + 0.5 * values * (1.0 - tangent * tangent) * COEF * (
        1.0 + 3.0 * CUBIC * values * values
    )


def depthwise(padded, taps):
    height = padded.shape[1] - 6
    width = padded.shape[2] - 6
    total = jnp.zeros((padded.shape[0], height, width, padded.shape[3]), jnp.float32)
    for row_tap in range(7):
        for col_tap in range(7):
            window = padded[:, row_tap : row_tap + height, col_tap : col_tap + width, :].astype(
                jnp.float32
            )
            total = total + window * taps[row_tap, col_tap]
    return total


def tap_grads(padded, upstream):
    height = upstream.shape[1]
    width = upstream.shape[2]
    rows_out = []
    for row_tap in range(7):
        line = []
        for col_tap in range(7):
            window = padded[:, row_tap : row_tap + height, col_tap : col_tap + width, :].astype(
                jnp.float32
            )
            line.append(jnp.sum(window * upstream, axis=(0, 1, 2)))
        rows_out.append(jnp.stack(line))
    return jnp.stack(rows_out)


def forward_layer(
    padded, current, taps, tap_bias, gain, shift, weight_in, bias_in, weight_out, bias_out, scale
):
    channels = current.shape[-1]
    mixed = (depthwise(padded, taps) + tap_bias).reshape(-1, channels)
    center = mixed - jnp.mean(mixed, -1, keepdims=True)
    rstd = lax.rsqrt(jnp.mean(center * center, -1, keepdims=True) + EPSILON)
    normed = center * rstd
    normal_low = (normed * gain + shift).astype(jnp.bfloat16)
    hidden = jnp.dot(normal_low, weight_in, preferred_element_type=jnp.float32) + bias_in
    activated = gelu_tanh(hidden).astype(jnp.bfloat16)
    branch = jnp.dot(activated, weight_out, preferred_element_type=jnp.float32) + bias_out
    result = current.reshape(-1, channels).astype(jnp.float32) + scale * branch
    result = result.astype(jnp.bfloat16).reshape(current.shape)
    return (result, (normed, rstd, normal_low, hidden, activated, branch))


def backward_layer(upstream, saved, gain, weight_in, weight_out, scale):
    normed, rstd, normal_low, hidden, activated, branch = saved
    contract_rows = (((0,), (0,)), ((), ()))
    contract_cols = (((1,), (1,)), ((), ()))
    grad_scale = jnp.sum(upstream * branch, 0)
    grad_branch = upstream * scale
    grad_bias_out = jnp.sum(grad_branch, 0)
    branch_low = grad_branch.astype(jnp.bfloat16)
    grad_weight_out = lax.dot_general(
        activated, branch_low, contract_rows, preferred_element_type=jnp.float32
    )
    grad_act = lax.dot_general(
        branch_low, weight_out, contract_cols, preferred_element_type=jnp.float32
    )
    grad_hidden = grad_act * gelu_slope(hidden)
    grad_bias_in = jnp.sum(grad_hidden, 0)
    hidden_low = grad_hidden.astype(jnp.bfloat16)
    grad_weight_in = lax.dot_general(
        normal_low, hidden_low, contract_rows, preferred_element_type=jnp.float32
    )
    grad_normal = lax.dot_general(
        hidden_low, weight_in, contract_cols, preferred_element_type=jnp.float32
    )
    grad_gain = jnp.sum(grad_normal * normed, 0)
    grad_shift = jnp.sum(grad_normal, 0)
    scaled = grad_normal * gain
    grad_mixed = rstd * (
        scaled
        - jnp.mean(scaled, -1, keepdims=True)
        - normed * jnp.mean(scaled * normed, -1, keepdims=True)
    )
    grad_tap_bias = jnp.sum(grad_mixed, 0)
    channel_grads = jnp.stack([grad_tap_bias, grad_gain, grad_shift, grad_bias_out, grad_scale])
    return (grad_mixed, grad_weight_in, grad_weight_out, grad_bias_in, channel_grads)


def reduce_weights(grad_in, grad_out):
    half_in, half_out = (
        sent_and_summed(grad_in.astype(jnp.bfloat16), "dp", 0),
        sent_and_summed(grad_out.astype(jnp.bfloat16), "dp", 1),
    )
    shard_in, shard_out = (
        total_of(half_in.astype(jnp.bfloat16), ("row", "col")),
        total_of(half_out.astype(jnp.bfloat16), ("row", "col")),
    )
    return (shard_in, shard_out)


def per_device(
    slides,
    cotangent,
    kernel,
    kernel_bias,
    norm_gain,
    norm_bias,
    weight_in,
    bias_in,
    weight_out,
    bias_out,
    layer_scale,
):
    layers = weight_in.shape[0]
    channels = slides.shape[-1]
    current = slides
    caches = []
    paddings = []
    fetched = []
    for which in range(layers):
        full_in, full_out = turned_gather((weight_in[which], weight_out[which]), "dp", (0, 1))
        fetched.append((full_in, full_out))
        padded = with_halo(current, (("row", 1), ("col", 2)), 3)
        current, cache = forward_layer(
            padded,
            current,
            kernel[which],
            kernel_bias[which],
            norm_gain[which],
            norm_bias[which],
            full_in,
            bias_in[which],
            full_out,
            bias_out[which],
            layer_scale[which],
        )
        caches.append(cache)
        paddings.append(padded)
    upstream = cotangent.astype(jnp.float32).reshape(-1, channels)
    grads_in = [None] * layers
    grads_out = [None] * layers
    grads_kernel = [None] * layers
    grads_channel = [None] * layers
    grads_bias = [None] * layers
    for which in reversed(range(layers)):
        full_in, full_out = fetched[which]
        grad_mixed, grad_in, grad_out, grad_bias, channel_grads = backward_layer(
            upstream, caches[which], norm_gain[which], full_in, full_out, layer_scale[which]
        )
        shaped = grad_mixed.reshape(slides.shape)
        rim = with_halo(shaped.astype(jnp.bfloat16), (("row", 1), ("col", 2)), 3).astype(
            shaped.dtype
        )
        local_taps = tap_grads(paddings[which], shaped)
        back = depthwise(rim, kernel[which][::-1, ::-1])
        upstream = upstream + back.reshape(-1, channels)
        grads_in[which], grads_out[which] = reduce_weights(grad_in, grad_out)
        grads_kernel[which], grads_channel[which], grads_bias[which] = lax.psum(
            (local_taps, channel_grads, grad_bias), ("row", "col", "dp")
        )
    grad_slides = upstream.astype(jnp.bfloat16).reshape(slides.shape)
    return (
        current,
        grad_slides,
        jnp.stack(grads_in),
        jnp.stack(grads_out),
        jnp.stack(grads_kernel),
        jnp.stack(grads_channel),
        jnp.stack(grads_bias),
    )


def solution(mesh):
    return jax.shard_map(
        per_device,
        mesh=mesh,
        in_specs=(
            P("dp", "row", "col", None),
            P("dp", "row", "col", None),
            P(),
            P(),
            P(),
            P(),
            P(None, "dp", None),
            P(),
            P(None, None, "dp"),
            P(),
            P(),
        ),
        out_specs=(
            P("dp", "row", "col", None),
            P("dp", "row", "col", None),
            P(None, "dp", None),
            P(None, None, "dp"),
            P(),
            P(),
            P(),
        ),
        check_vma=False,
    )
```

profile of v0, /device:TPU:1, one launch (start us, length us, event | category | flops | bytes accessed | tf_op | source)
XLA Modules:
  0.0 646.8 jit_solution(13903822285871508626)
XLA Ops:
  38.8 11.4 %fusion.385 = (f32[16,32]{1,0:T(8,128)S(1)}, f32[1,16,32,512]{3,2,1,0:T(8,128)S(1)}) fusion(f32[512]{0:T(512)S(1)} %bitcast.634, f32[512]{0:T(512)S(1)} %bitcast.461, bf16[1,22,3,512]{3,2,1,0:T(4,128)(2,1)S(1)} %collective-permute-done.3, bf16[1,22,32,512]{3,2,1,0:T(8,128)(2,1)S(1)} %get-tuple-element.312, f32[512]{0:T(512)S(1)} %bitcast.463, ...), kind=kLoop, calls=%fused_computation.850 | loop fusion | flops 71826944 | bytes 5679104 | tf_op jit(solution)/shard_map/reduce_sum | solution.py:122
  52.8 24.5 %all-gather.3.cloned.1.call-done = bf16[512,4096]{0,1:T(8,128)(2,1)} async-done(((bf16[256,4096]{0,1:T(8,128)(2,1)}), bf16[512,4096]{0,1:T(8,128)(2,1)}) %all-gather.3.cloned.1.call-update) | async-done | bytes 4194320 | tf_op jit(solution)/shard_map/all_gather | solution.py:54
  101.1 9.2 %fusion.383 = (f32[16,32]{1,0:T(8,128)S(1)}, f32[1,16,32,512]{3,2,1,0:T(8,128)}) fusion(f32[512]{0:T(512)S(1)} %bitcast.650, f32[512]{0:T(512)S(1)} %bitcast.529, bf16[1,22,35,512]{3,2,1,0:T(8,128)(2,1)S(1)} %get-tuple-element.193, f32[512]{0:T(512)S(1)} %bitcast.531, f32[512]{0:T(512)S(1)} %bitcast.533, f32[512]{0:T(512)S(1)} %bitcast.536, ...), kind=kLoop, calls=%fused_computation.849 | loop fusion | flops 40369664 | bytes 23894016 | tf_op jit(solution)/shard_map/reduce_sum | solution.py:122
  114.5 24.6 %all-gather.5.cloned.1.call-done = bf16[512,4096]{0,1:T(8,128)(2,1)} async-done(((bf16[256,4096]{0,1:T(8,128)(2,1)}), bf16[512,4096]{0,1:T(8,128)(2,1)}) %all-gather.5.cloned.1.call-update) | async-done | bytes 4194320 | tf_op jit(solution)/shard_map/all_gather | solution.py:54
  176.3 10.3 %multiply_reduce_fusion.2 = (f32[512]{0:T(512)}, f32[512]{0:T(512)}, f32[1,16,32,512]{3,2,1,0:T(8,128)S(1)}) fusion(bf16[1,16,32,512]{3,2,1,0:T(8,128)(2,1)} %param.12, f32[512]{0:T(512)} %bitcast.647, f32[512]{0:T(512)} %bitcast.629, f32[512]{0:T(512)S(1)} %bitcast.528, f32[1,22,38,512]{3,2,1,0:T(8,128)S(1)} %maximum_convert_fusion.2, f32[512]{0:T(512)} %bitcast.566, ...), kind=kLoop, calls=%fused_computation.682 | loop fusion | flops 26999808 | bytes 53061632 | tf_op jit(solution)/shard_map/reduce_sum | solution.py:140
  191.1 8.7 %all-to-all-done.3 = bf16[2,256,2048]{2,1,0:T(8,128)(2,1)} async-done(((bf16[2,256,2048]{2,1,0:T(8,128)(2,1)}), bf16[2,256,2048]{2,1,0:T(8,128)(2,1)}, u32[]{:S(2)}, u32[]{:S(2)}) %all-to-all-start.3) | async-done | bytes 2097184 | tf_op jit(solution)/shard_map/all_to_all | solution.py:18
  204.7 6.9 %fusion.407 = (f32[2048]{0:T(1024)}, bf16[512,2048]{1,0:T(8,128)(2,1)S(1)}) fusion(f32[512,2048]{1,0:T(8,128)} %copy-done.9, f32[2048]{0:T(1024)S(1)} %bitcast.707, bf16[512,512]{1,0:T(8,128)(2,1)} %get-tuple-element.186, bf16[512,4096]{0,1:T(8,128)(2,1)} %all-gather.3.cloned.1.call-done), kind=kOutput, calls=%fused_computation.871 | convolution fusion | flops 1095759872 | bytes 8929280 | tf_op jit(solution)/shard_map/dot_general | solution.py:145
  215.5 13.3 %all-to-all-done.9 = bf16[2,2048,256]{1,2,0:T(8,128)(2,1)} async-done(((bf16[2,2048,256]{1,2,0:T(8,128)(2,1)}), bf16[2,2048,256]{1,2,0:T(8,128)(2,1)}, u32[]{:S(2)}, u32[]{:S(2)}) %all-to-all-start.9) | async-done | bytes 2097184 | tf_op jit(solution)/shard_map/all_to_all | solution.py:18
  241.0 16.1 %all-to-all-done = bf16[2,256,2048]{2,1,0:T(8,128)(2,1)} async-done(((bf16[2,256,2048]{2,1,0:T(8,128)(2,1)}), bf16[2,256,2048]{2,1,0:T(8,128)(2,1)}, u32[]{:S(2)}, u32[]{:S(2)}) %all-to-all-start) | async-done | bytes 2097184 | tf_op jit(solution)/shard_map/all_to_all | solution.py:18
  276.6 7.9 %all-to-all-done.6 = bf16[2,2048,256]{1,2,0:T(8,128)(2,1)} async-done(((bf16[2,2048,256]{1,2,0:T(8,128)(2,1)}), bf16[2,2048,256]{1,2,0:T(8,128)(2,1)}, u32[]{:S(2)}, u32[]{:S(2)}) %all-to-all-start.6) | async-done | bytes 2097184 | tf_op jit(solution)/shard_map/all_to_all | solution.py:18
  284.4 12.6 %all-to-all-start.4 = ((bf16[64,4,2048]{2,1,0:T(4,128)(2,1)}), bf16[64,4,2048]{2,1,0:T(4,128)(2,1)S(1)}, u32[]{:S(2)}, u32[]{:S(2)}) async-start(bf16[64,4,2048]{2,1,0:T(4,128)(2,1)} %reshape.942), calls=%async_computation.4 | async-start | bytes 2097152 | tf_op jit(solution)/shard_map/all_to_all | solution.py:18
  306.4 9.8 %all-to-all-done.4 = bf16[64,4,2048]{2,1,0:T(4,128)(2,1)S(1)} async-done(((bf16[64,4,2048]{2,1,0:T(4,128)(2,1)}), bf16[64,4,2048]{2,1,0:T(4,128)(2,1)S(1)}, u32[]{:S(2)}, u32[]{:S(2)}) %all-to-all-start.4) | async-done | bytes 1048608 | tf_op jit(solution)/shard_map/all_to_all | solution.py:18
  334.1 7.6 %all-to-all-done.10 = bf16[64,32,256]{2,1,0:T(8,128)(2,1)S(1)} async-done(((bf16[64,32,256]{2,1,0:T(8,128)(2,1)}), bf16[64,32,256]{2,1,0:T(8,128)(2,1)S(1)}, u32[]{:S(2)}, u32[]{:S(2)}) %all-to-all-start.10) | async-done | bytes 1048608 | tf_op jit(solution)/shard_map/all_to_all | solution.py:18
  341.7 5.8 all-to-all-start.1
  366.6 9.8 %all-to-all-start.7 = ((bf16[64,32,256]{2,1,0:T(8,128)(2,1)}), bf16[64,32,256]{2,1,0:T(8,128)(2,1)}, u32[]{:S(2)}, u32[]{:S(2)}) async-start(bf16[64,32,256]{2,1,0:T(8,128)(2,1)} %bitcast.446), calls=%async_computation.7 | async-start | bytes 2097152 | tf_op jit(solution)/shard_map/all_to_all | solution.py:18
  387.6 7.8 %all-to-all-done.7 = bf16[64,32,256]{2,1,0:T(8,128)(2,1)} async-done(((bf16[64,32,256]{2,1,0:T(8,128)(2,1)}), bf16[64,32,256]{2,1,0:T(8,128)(2,1)}, u32[]{:S(2)}, u32[]{:S(2)}) %all-to-all-start.7) | async-done | bytes 1048608 | tf_op jit(solution)/shard_map/all_to_all | solution.py:18
  397.0 5.4 all-to-all-start.5
  413.9 7.5 %all-to-all-done.5 = bf16[64,4,2048]{2,1,0:T(4,128)(2,1)S(1)} async-done(((bf16[64,4,2048]{2,1,0:T(4,128)(2,1)}), bf16[64,4,2048]{2,1,0:T(4,128)(2,1)S(1)}, u32[]{:S(2)}, u32[]{:S(2)}) %all-to-all-start.5) | async-done | bytes 1048608 | tf_op jit(solution)/shard_map/all_to_all | solution.py:29
  429.5 17.4 %all-to-all-done.11 = bf16[64,32,256]{2,1,0:T(8,128)(2,1)S(1)} async-done(((bf16[64,32,256]{2,1,0:T(8,128)(2,1)}), bf16[64,32,256]{2,1,0:T(8,128)(2,1)S(1)}, u32[]{:S(2)}, u32[]{:S(2)}) %all-to-all-start.11) | async-done | bytes 1048608 | tf_op jit(solution)/shard_map/all_to_all | solution.py:29
  448.4 5.9 all-to-all-start.2
  455.2 70.8 %all-reduce = (f32[1,5,512]{2,1,0:T(8,128)S(1)}, f32[1,5,512]{2,1,0:T(8,128)S(1)}, f32[1,2048]{1,0:T(1,128)S(1)}, f32[1,2048]{1,0:T(1,128)S(1)}) all-reduce(f32[1,5,512]{2,1,0:T(8,128)S(1)} %bitcast.457, f32[1,5,512]{2,1,0:T(8,128)S(1)} %bitcast.458, ...), channel_id=1, replica_groups=mesh['row'=16,'col'=4,'dp'=2] {'row','col','dp'}, use_global_device_ids=true, to_apply=%region_127.128 | all-reduce | flops 9216 | bytes 73728 | tf_op jit(solution)/shard_map/psum | solution.py:239
  533.8 70.9 %all-reduce.4.cloned.1.call-done = (f32[1,7,7,512]{3,2,1,0:T(8,128)}, f32[1,7,7,512]{3,2,1,0:T(8,128)}) async-done(((f32[1,7,7,512]{3,2,1,0:T(8,128)}, f32[1,7,7,512]{3,2,1,0:T(8,128)}), (f32[1,7,7,512]{3,2,1,0:T(8,128)}, f32[1,7,7,512]{3,2,1,0:T(8,128)})) %all-reduce.4.cloned.1.call-update) | async-done | bytes 200720 | tf_op jit(solution)/shard_map/psum | solution.py:239
  610.4 7.1 %all-to-all-start.8 = ((bf16[64,32,256]{2,1,0:T(8,128)(2,1)}), bf16[64,32,256]{2,1,0:T(8,128)(2,1)}, u32[]{:S(2)}, u32[]{:S(2)}) async-start(bf16[64,32,256]{2,1,0:T(8,128)(2,1)} %broadcast_in_dim.10), calls=%async_computation.8 | async-start | bytes 2097152 | tf_op jit(solution)/shard_map/all_to_all | solution.py:29
  617.8 9.0 %fusion.228 = bf16[1,16,32,512]{3,2,1,0:T(8,128)(2,1)} fusion(f32[1,22,38,512]{3,2,1,0:T(8,128)S(1)} %maximum_convert_fusion.3, f32[1,16,32,512]{3,2,1,0:T(8,128)} %copy-done.21, bf16[1,16,32,512]{3,2,1,0:T(8,128)(2,1)S(1)} %copy-done.20, f32[512]{0:T(512)S(1)} %bitcast.462, f32[512]{0:T(512)S(1)} %bitcast.464, f32[512]{0:T(512)S(1)} %bitcast.466, ...), kind=kLoop, calls=%fused_computation.473 | loop fusion | flops 26476544 | bytes 53577728 | tf_op jit(solution)/shard_map/convert_element_type | solution.py:242
  (587 shorter events, 248.7 us)
Async XLA Ops:
  7.2 70.1 %all-gather.3.cloned.1.call-start = ((), (), s32[]{:S(2)}) async-start(), calls=%async_computation.12 | async-start | bytes 6291456 | tf_op jit(solution)/shard_map/all_gather | solution.py:54
  14.9 124.2 %all-gather.5.cloned.1.call-start = ((), (), s32[]{:S(2)}) async-start(), calls=%async_computation.13 | async-start | bytes 6291456 | tf_op jit(solution)/shard_map/all_gather | solution.py:54
  15.0 16.4 %collective-permute-start = (bf16[1,3,32,512]{3,2,1,0:T(8,128)(2,1)S(1)}, bf16[1,3,32,512]{3,2,1,0:T(8,128)(2,1)S(1)}, u32[]{:S(2)}, u32[]{:S(2)}) collective-permute-start(bf16[1,3,32,512]{3,2,1,0:T(8,128)(2,1)S(1)} %get-tuple-element.208), channel_id=1, source_target_pairs={{0,8},{8,16},{16,24},{24,32},{32,40},{40,48},{48,56},{56,64},{64,7... | collective-permute-start | bytes 294920 | tf_op jit(solution)/shard_map/ppermute | solution.py:69
  19.6 12.1 %collective-permute-start.1 = (bf16[1,3,32,512]{3,2,1,0:T(8,128)(2,1)S(1)}, bf16[1,3,32,512]{3,2,1,0:T(8,128)(2,1)S(1)}, u32[]{:S(2)}, u32[]{:S(2)}) collective-permute-start(bf16[1,3,32,512]{3,2,1,0:T(8,128)(2,1)S(1)} %get-tuple-element.207), channel_id=1, source_target_pairs={{8,0},{16,8},{24,16},{32,24},{40,32},{48,40},{56,48},{64,56},{72,6... | collective-permute-start | bytes 294920 | tf_op jit(solution)/shard_map/ppermute | solution.py:72
  150.9 9.3 %collective-permute-start.9 = (bf16[1,3,32,512]{3,2,1,0:T(8,128)(2,1)S(1)}, bf16[1,3,32,512]{3,2,1,0:T(8,128)(2,1)S(1)}, u32[]{:S(2)}, u32[]{:S(2)}) collective-permute-start(bf16[1,3,32,512]{3,2,1,0:T(8,128)(2,1)S(1)} %get-tuple-element.201), channel_id=1, source_target_pairs={{8,0},{16,8},{24,16},{32,24},{40,32},{48,40},{56,48},{64,56},{72,6... | collective-permute-start | bytes 294920 | tf_op jit(solution)/shard_map/ppermute | solution.py:72
  160.9 13.9 %collective-permute-start.11 = (bf16[1,22,3,512]{3,2,1,0:T(4,128)(2,1)}, bf16[1,22,3,512]{3,2,1,0:T(4,128)(2,1)}, u32[]{:S(2)}, u32[]{:S(2)}) collective-permute-start(bf16[1,22,3,512]{3,2,1,0:T(4,128)(2,1)} %get-tuple-element.191), channel_id=1, source_target_pairs={{2,0},{4,2},{6,4},{3,1},{5,3},{7,5},{10,8},{12,10},{14,12},{11,9},... | collective-permute-start | bytes 202760 | tf_op jit(solution)/shard_map/ppermute | solution.py:72
  162.1 12.6 %collective-permute-start.10 = (bf16[1,22,3,512]{3,2,1,0:T(4,128)(2,1)}, bf16[1,22,3,512]{3,2,1,0:T(4,128)(2,1)}, u32[]{:S(2)}, u32[]{:S(2)}) collective-permute-start(bf16[1,22,3,512]{3,2,1,0:T(4,128)(2,1)} %get-tuple-element.190), channel_id=1, source_target_pairs={{0,2},{2,4},{4,6},{1,3},{3,5},{5,7},{8,10},{10,12},{12,14},{9,11},... | collective-permute-start | bytes 202760 | tf_op jit(solution)/shard_map/ppermute | solution.py:69
  169.4 30.3 %all-to-all-start.3 = ((bf16[2,256,2048]{2,1,0:T(8,128)(2,1)}), bf16[2,256,2048]{2,1,0:T(8,128)(2,1)}, u32[]{:S(2)}, u32[]{:S(2)}) async-start(bf16[2,256,2048]{2,1,0:T(8,128)(2,1)} %bitcast.453), calls=%async_computation.3 | async-start | bytes 4194304 | tf_op jit(solution)/shard_map/all_to_all | solution.py:18
  199.8 29.1 %all-to-all-start.9 = ((bf16[2,2048,256]{1,2,0:T(8,128)(2,1)}), bf16[2,2048,256]{1,2,0:T(8,128)(2,1)}, u32[]{:S(2)}, u32[]{:S(2)}) async-start(bf16[2,2048,256]{1,2,0:T(8,128)(2,1)} %bitcast.451), calls=%async_computation.9 | async-start | bytes 4194304 | tf_op jit(solution)/shard_map/all_to_all | solution.py:18
  228.8 28.3 %all-to-all-start = ((bf16[2,256,2048]{2,1,0:T(8,128)(2,1)}), bf16[2,256,2048]{2,1,0:T(8,128)(2,1)}, u32[]{:S(2)}, u32[]{:S(2)}) async-start(bf16[2,256,2048]{2,1,0:T(8,128)(2,1)} %bitcast.454), calls=%async_computation | async-start | bytes 4194304 | tf_op jit(solution)/shard_map/all_to_all | solution.py:18
  257.2 27.3 %all-to-all-start.6 = ((bf16[2,2048,256]{1,2,0:T(8,128)(2,1)}), bf16[2,2048,256]{1,2,0:T(8,128)(2,1)}, u32[]{:S(2)}, u32[]{:S(2)}) async-start(bf16[2,2048,256]{1,2,0:T(8,128)(2,1)} %bitcast.452), calls=%async_computation.6 | async-start | bytes 4194304 | tf_op jit(solution)/shard_map/all_to_all | solution.py:18
  284.4 31.7 %all-to-all-start.4 = ((bf16[64,4,2048]{2,1,0:T(4,128)(2,1)}), bf16[64,4,2048]{2,1,0:T(4,128)(2,1)S(1)}, u32[]{:S(2)}, u32[]{:S(2)}) async-start(bf16[64,4,2048]{2,1,0:T(4,128)(2,1)} %reshape.942), calls=%async_computation.4 | async-start | bytes 2097152 | tf_op jit(solution)/shard_map/all_to_all | solution.py:18
  317.2 24.4 %all-to-all-start.10 = ((bf16[64,32,256]{2,1,0:T(8,128)(2,1)}), bf16[64,32,256]{2,1,0:T(8,128)(2,1)S(1)}, u32[]{:S(2)}, u32[]{:S(2)}) async-start(bf16[64,32,256]{2,1,0:T(8,128)(2,1)} %bitcast.447), calls=%async_computation.10 | async-start | bytes 2097152 | tf_op jit(solution)/shard_map/all_to_all | solution.py:18
  341.7 24.9 %all-to-all-start.1 = ((bf16[64,4,2048]{2,1,0:T(4,128)(2,1)}), bf16[64,4,2048]{2,1,0:T(4,128)(2,1)}, u32[]{:S(2)}, u32[]{:S(2)}) async-start(bf16[64,4,2048]{2,1,0:T(4,128)(2,1)} %reshape.940), calls=%async_computation.1 | async-start | bytes 2097152 | tf_op jit(solution)/shard_map/all_to_all | solution.py:18
  350.1 177.5 %collective-permute-start.13 = (bf16[1,3,32,512]{3,2,1,0:T(8,128)(2,1)}, bf16[1,3,32,512]{3,2,1,0:T(8,128)(2,1)}, u32[]{:S(2)}, u32[]{:S(2)}) collective-permute-start(bf16[1,3,32,512]{3,2,1,0:T(8,128)(2,1)} %get-tuple-element.199), channel_id=1, source_target_pairs={{8,0},{16,8},{24,16},{32,24},{40,32},{48,40},{56,48},{64,56},{72,6... | collective-permute-start | bytes 294920 | tf_op jit(solution)/shard_map/ppermute | solution.py:72
  352.7 174.9 %collective-permute-start.12 = (bf16[1,3,32,512]{3,2,1,0:T(8,128)(2,1)}, bf16[1,3,32,512]{3,2,1,0:T(8,128)(2,1)}, u32[]{:S(2)}, u32[]{:S(2)}) collective-permute-start(bf16[1,3,32,512]{3,2,1,0:T(8,128)(2,1)} %get-tuple-element.198), channel_id=1, source_target_pairs={{0,8},{8,16},{16,24},{24,32},{32,40},{40,48},{48,56},{56,64},{64,7... | collective-permute-start | bytes 294920 | tf_op jit(solution)/shard_map/ppermute | solution.py:69
  366.6 28.8 %all-to-all-start.7 = ((bf16[64,32,256]{2,1,0:T(8,128)(2,1)}), bf16[64,32,256]{2,1,0:T(8,128)(2,1)}, u32[]{:S(2)}, u32[]{:S(2)}) async-start(bf16[64,32,256]{2,1,0:T(8,128)(2,1)} %bitcast.446), calls=%async_computation.7 | async-start | bytes 2097152 | tf_op jit(solution)/shard_map/all_to_all | solution.py:18
  397.0 24.5 %all-to-all-start.5 = ((bf16[64,4,2048]{2,1,0:T(4,128)(2,1)}), bf16[64,4,2048]{2,1,0:T(4,128)(2,1)S(1)}, u32[]{:S(2)}, u32[]{:S(2)}) async-start(bf16[64,4,2048]{2,1,0:T(4,128)(2,1)} %broadcast_in_dim.9), calls=%async_computation.5 | async-start | bytes 2097152 | tf_op jit(solution)/shard_map/all_to_all | solution.py:29
  422.6 24.2 %all-to-all-start.11 = ((bf16[64,32,256]{2,1,0:T(8,128)(2,1)}), bf16[64,32,256]{2,1,0:T(8,128)(2,1)S(1)}, u32[]{:S(2)}, u32[]{:S(2)}) async-start(bf16[64,32,256]{2,1,0:T(8,128)(2,1)} %broadcast_in_dim.11), calls=%async_computation.11 | async-start | bytes 2097152 | tf_op jit(solution)/shard_map/all_to_all | solution.py:29
  448.4 160.9 %all-to-all-start.2 = ((bf16[64,4,2048]{2,1,0:T(4,128)(2,1)}), bf16[64,4,2048]{2,1,0:T(4,128)(2,1)}, u32[]{:S(2)}, u32[]{:S(2)}) async-start(bf16[64,4,2048]{2,1,0:T(4,128)(2,1)} %broadcast_in_dim.8), calls=%async_computation.2 | async-start | bytes 2097152 | tf_op jit(solution)/shard_map/all_to_all | solution.py:29
  454.2 150.5 %all-reduce.4.cloned.1.call-start = ((), (), s32[]{:S(2)}) async-start(), calls=%async_computation.14 | async-start | bytes 458752 | tf_op jit(solution)/shard_map/psum | solution.py:239
  528.5 78.1 %collective-permute-start.15 = (bf16[1,22,3,512]{3,2,1,0:T(4,128)(2,1)S(1)}, bf16[1,22,3,512]{3,2,1,0:T(4,128)(2,1)S(1)}, u32[]{:S(2)}, u32[]{:S(2)}) collective-permute-start(bf16[1,22,3,512]{3,2,1,0:T(4,128)(2,1)S(1)} %get-tuple-element.189), channel_id=1, source_target_pairs={{2,0},{4,2},{6,4},{3,1},{5,3},{7,5},{10,8},{12,10},{14,12},{11,9},... | collective-permute-start | bytes 202760 | tf_op jit(solution)/shard_map/ppermute | solution.py:72
  529.8 76.8 %collective-permute-start.14 = (bf16[1,22,3,512]{3,2,1,0:T(4,128)(2,1)S(1)}, bf16[1,22,3,512]{3,2,1,0:T(4,128)(2,1)S(1)}, u32[]{:S(2)}, u32[]{:S(2)}) collective-permute-start(bf16[1,22,3,512]{3,2,1,0:T(4,128)(2,1)S(1)} %get-tuple-element.188), channel_id=1, source_target_pairs={{0,2},{2,4},{4,6},{1,3},{3,5},{5,7},{8,10},{10,12},{12,14},{9,11},... | collective-permute-start | bytes 202760 | tf_op jit(solution)/shard_map/ppermute | solution.py:69
  610.4 25.9 %all-to-all-start.8 = ((bf16[64,32,256]{2,1,0:T(8,128)(2,1)}), bf16[64,32,256]{2,1,0:T(8,128)(2,1)}, u32[]{:S(2)}, u32[]{:S(2)}) async-start(bf16[64,32,256]{2,1,0:T(8,128)(2,1)} %broadcast_in_dim.10), calls=%async_computation.8 | async-start | bytes 2097152 | tf_op jit(solution)/shard_map/all_to_all | solution.py:29
  (212 other events, 6746.2 us)
Sparse Core Ops, SparseCore 0:
  15.0 62.2 all-gather.2
  78.9 60.1 all-gather.4
  460.6 144.1 all-reduce.3
where the time goes:
time: 657 us; the launch traced here: 647 us
  waiting for transfers between devices  229 us (35%)
  starting transfers between devices  123 us (19%)
  other arithmetic  115 us (18%)
  blocking collectives  70.8 us (11%)
  local copies, waits for them, and re-layouts  49.2 us (7%)
  matrix products  42.8 us (7%)
  between operations  17.6 us (3%)
    all_to_all x8, waiting for transfers between devices, sent_and_summed(): pieces = lax.all_to_all(cut_along(shard, dim, size), axis, 0, 0, tiled=True)  72.5 us
    psum x1, waiting for transfers between devices, per_device(): lax.psum((local_taps, channel_grads, grad_bias), ('row', 'col', 'dp'))  70.9 us
    psum x1, blocking collectives, per_device(): lax.psum((local_taps, channel_grads, grad_bias), ('row', 'col', 'dp'))  70.8 us
    all_to_all x8, starting transfers between devices, sent_and_summed(): pieces = lax.all_to_all(cut_along(shard, dim, size), axis, 0, 0, tiled=True)  53.7 us
    all_gather x2, waiting for transfers between devices, turned_gather(): result = lax.all_gather(both, axis, axis=0, tiled=True)  49.1 us
    ppermute x8, starting transfers between devices, with_halo(): lax.ppermute(lax.slice_in_dim(block, block.shape[dim] - width, None, axis...  29.9 us
    all_to_all x4, waiting for transfers between devices, copy_for_each(): return lax.all_to_all(copies, axis, split_axis=0, concat_axis=0, tiled=True)  29.4 us
    reduce_sum x9, other arithmetic, tap_grads(): line.append(jnp.sum(window * upstream, axis=(0, 1, 2)))  29.3 us
  transfers between devices with their start and end apart: 31, of which 18 were waited for; matrix products, arithmetic and copies ran while one was open for 27% of the time, Pallas kernels for 0%

commit v1 on v0

v1 whole, which is shorter than its diff:
```python
import functools

import jax
import jax.numpy as jnp
from jax import lax
from jax.experimental import pallas as pl
from jax.experimental.pallas import tpu as pltpu
from jax.sharding import PartitionSpec as P

COEF = 0.7978845608028654
CUBIC = 0.044715
EPSILON = 1e-06

MESH = pl.DeviceIdType.MESH
BF = jnp.bfloat16
F32 = jnp.float32


class Place:
    def __init__(self):
        row = lax.axis_index("row")
        self.z = lax.axis_index("col")
        self.half = lax.axis_index("dp")
        self.core = lax.rem(row, 2)
        self.y = lax.rem(lax.div(row, 2), 4)
        self.x = lax.div(row, 8) * 2 + self.half

    def device(self, x=None, y=None, z=None, core=None):
        x = self.x if x is None else x
        y = self.y if y is None else y
        z = self.z if z is None else z
        core = self.core if core is None else core
        return {"row": (lax.div(x, 2) * 4 + y) * 2 + core, "col": z, "dp": lax.rem(x, 2)}

    def along(self, axis, offset):
        value = lax.rem(getattr(self, axis) + offset, 4)
        return value, self.device(**{axis: value})

    def sibling(self):
        return self.device(core=1 - self.core)


def meet(partners):
    barrier = pltpu.get_barrier_semaphore()
    for partner in partners:
        pl.semaphore_signal(barrier, inc=1, device_id=partner, device_id_type=MESH)
    pl.semaphore_wait(barrier, len(partners))


def part(start, size):
    if isinstance(start, int):
        return pl.ds(start, size)
    return pl.ds(pl.multiple_of(start, size), size)


def remote(src, dst, send, recv, target):
    return pltpu.make_async_remote_copy(
        src_ref=src, dst_ref=dst, send_sem=send, recv_sem=recv, device_id=target, device_id_type=MESH
    )


ORDERS = (("y", "z"), ("z", "y"))


class WeightIn:
    received = (2, 128, 2048)
    first = (2, 64, 512)
    second = (2, 64, 128)
    third = (64, 128)

    def offered(grad, half, core):
        return grad.at[part(half * 256 + core * 128, 128), :]

    def cut(got, turn, index):
        return got.at[:, turn * 64 : turn * 64 + 64, part(index * 512, 512)]

    def cut_again(block, index):
        return block.at[:, :, part(index * 128, 128)]

    def placed(final, core, turn, one, two):
        return final.at[part(core * 128 + turn * 64, 64), part(one * 512 + two * 128, 128)]

    def line(final, core, turn, one):
        return final.at[part(core * 128 + turn * 64, 64), part(one * 512, 512)]

    def of_core(final, core):
        return final.at[part(core * 128, 128), :]


class WeightOut:
    received = (2, 2048, 128)
    first = (2, 256, 128)
    second = (2, 64, 128)
    third = (64, 128)

    def offered(grad, half, core):
        return grad.at[:, part(half * 256 + core * 128, 128)]

    def cut(got, turn, index):
        return got.at[:, part(turn * 1024 + index * 256, 256), :]

    def cut_again(block, index):
        return block.at[:, part(index * 64, 64), :]

    def placed(final, core, turn, one, two):
        return final.at[part(turn * 1024 + one * 256 + two * 64, 64), part(core * 128, 128)]

    def line(final, core, turn, one):
        return final.at[part(turn * 1024 + one * 256, 256), part(core * 128, 128)]

    def of_core(final, core):
        return final.at[:, part(core * 128, 128)]


class Small:
    received = (1, 64, 512)
    first = (1, 32, 128)
    second = (1, 8, 128)
    third = (8, 128)

    def offered(grad, half, core):
        return grad.at[part(core * 64, 64), :]

    def cut(got, turn, index):
        return got.at[:, turn * 32 : turn * 32 + 32, part(index * 128, 128)]

    def cut_again(block, index):
        return block.at[:, part(index * 8, 8), :]

    def placed(final, core, turn, one, two):
        return final.at[part(core * 64 + turn * 32 + two * 8, 8), part(one * 128, 128)]

    def line(final, core, turn, one):
        return final.at[part(core * 64 + turn * 32, 32), part(one * 128, 128)]

    def of_core(final, core):
        return final.at[part(core * 64, 64), :]


class Reduction:
    def __init__(self, me, kind, grad, final, bufs, sems):
        self.me, self.kind, self.grad, self.final = me, kind, grad, final
        self.got, self.r1, self.b1, self.r2, self.b2, self.r3 = bufs
        self.sems = sems
        self.halves = 1 if kind is Small else 2
        self.copies = []

    def sem(self, way, turn, step, slot):
        return self.sems.at[way, (turn * 7 + step) * 4 + slot]

    def go(self, src, dst, turn, step, send_slot, recv_slot, target):
        copy = remote(
            src, dst, self.sem(0, turn, step, send_slot), self.sem(1, turn, step, recv_slot), target
        )
        copy.start()
        self.copies.append(copy)

    def landed(self, dst, turn, step, slot):
        remote(
            dst, dst, self.sem(0, turn, step, slot), self.sem(1, turn, step, slot), self.me.sibling()
        ).wait_recv()

    def core_start(self):
        for half in range(self.halves):
            src = self.kind.offered(self.grad, half, 1 - self.me.core)
            self.go(src, self.got.at[half], 0, 0, half, half, self.me.sibling())

    def core_finish(self):
        for half in range(self.halves):
            self.landed(self.got.at[half], 0, 0, half)
            own = self.kind.offered(self.grad, half, self.me.core)
            total = own[...].astype(F32) + self.got[half].astype(F32)
            self.got[half] = total.astype(self.got.dtype)

    def block(self, turn, step, index):
        if step == 0:
            return self.kind.cut(self.got, turn, index)
        return self.kind.cut_again(self.b1.at[turn], index)

    def split_start(self, step):
        target = (self.r1, self.r2)[step]
        for turn in range(2):
            for offset in (1, 3, 2):
                index, device = self.me.along(ORDERS[turn][step], offset)
                self.go(
                    self.block(turn, step, index),
                    target.at[turn, offset - 1],
                    turn,
                    1 + step,
                    offset,
                    offset,
                    device,
                )

    def split_finish(self, step):
        target, result = ((self.r1, self.b1), (self.r2, self.b2))[step]
        for turn in range(2):
            index = getattr(self.me, ORDERS[turn][step])
            total = self.block(turn, step, index)[...].astype(F32)
            for offset in (1, 3, 2):
                self.landed(target.at[turn, offset - 1], turn, 1 + step, offset)
                total = total + target[turn, offset - 1].astype(F32)
            result[turn] = total.astype(result.dtype)

    def across_start(self):
        for turn in range(2):
            block = self.b2.at[turn]
            for offset in (1, 3, 2):
                index, device = self.me.along("x", offset)
                src = block.at[lax.rem(index, 2) if self.halves == 2 else 0]
                self.go(src, self.r3.at[turn, self.me.x], turn, 3, offset, self.me.x, device)
            self.r3[turn, self.me.x] = block[self.me.half if self.halves == 2 else 0]

    def across_finish(self):
        me = self.me
        for turn in range(2):
            for offset in (1, 3, 2):
                index, _ = me.along("x", offset)
                self.landed(self.r3.at[turn, index], turn, 3, index)
            total = self.r3[turn, 0].astype(F32)
            for index in range(1, 4):
                total = total + self.r3[turn, index].astype(F32)
            one, two = (getattr(me, axis) for axis in ORDERS[turn])
            block = self.kind.placed(self.final, me.core, turn, one, two)
            block[...] = total.astype(self.final.dtype)

    def join_start(self, step):
        me = self.me
        for turn in range(2):
            one, two = (getattr(me, axis) for axis in ORDERS[turn])
            for offset in (1, 3, 2):
                _, device = me.along(ORDERS[turn][step], offset)
                if step == 1:
                    block = self.kind.placed(self.final, me.core, turn, one, two)
                else:
                    block = self.kind.line(self.final, me.core, turn, one)
                self.go(block, block, turn, 5 - step, offset, offset, device)

    def join_finish(self, step):
        me = self.me
        for turn in range(2):
            one, two = (getattr(me, axis) for axis in ORDERS[turn])
            for offset in (1, 3, 2):
                source = lax.rem((two if step == 1 else one) + 4 - offset, 4)
                if step == 1:
                    block = self.kind.placed(self.final, me.core, turn, one, source)
                else:
                    block = self.kind.line(self.final, me.core, turn, source)
                self.landed(block, turn, 5 - step, offset)

    def share_start(self):
        block = self.kind.of_core(self.final, self.me.core)
        self.go(block, block, 0, 6, 0, 0, self.me.sibling())

    def share_finish(self):
        block = self.kind.of_core(self.final, 1 - self.me.core)
        self.landed(block, 0, 6, 0)

    def drain(self):
        for copy in self.copies:
            copy.wait_send()


def reduction_scratch(kind):
    dtype = F32 if kind is Small else BF
    return [
        pltpu.VMEM(kind.received, dtype),
        pltpu.VMEM((2, 3, *kind.first), dtype),
        pltpu.VMEM((2, *kind.first), dtype),
        pltpu.VMEM((2, 3, *kind.second), dtype),
        pltpu.VMEM((2, *kind.second), dtype),
        pltpu.VMEM((2, 4, *kind.third), dtype),
        pltpu.SemaphoreType.DMA((2, 56)),
    ]


UNITS = ((Small, None), (WeightOut, 1), (WeightIn, 1), (WeightOut, 0), (WeightIn, 0))


class Gather:
    def __init__(self, me, shard_in, shard_out, full_in, full_out, sems):
        self.me = me
        self.shards = (shard_in, shard_out)
        self.full = (full_in, full_out)
        self.local, self.send, self.recv, self.send_core, self.recv_core = sems
        self.sides = (me.along("x", 1)[1], me.along("x", 3)[1])
        self.copies = []

    def block(self, which, kind, half, core, side):
        full = self.full[kind].at[which]
        if kind == 0:
            return full.at[part(half * 256 + core * 128 + side * 64, 64), :]
        return full.at[part(core * 1024 + side * 512, 512), part(half * 256, 256)]

    def place(self, which, kind):
        half = part(self.me.half * 256, 256)
        full = self.full[kind].at[which]
        own = full.at[half, :] if kind == 0 else full.at[:, half]
        return pltpu.make_async_copy(self.shards[kind].at[which], own, self.local.at[which, kind])

    def hop(self, which, kind, half, core, side, across):
        block = self.block(which, kind, half, core, side)
        if across:
            sems, target = (self.send, self.recv), self.sides[side]
        else:
            sems, target = (self.send_core, self.recv_core), self.me.sibling()
        return remote(block, block, *(s.at[which, kind, side] for s in sems), target)

    def start(self, which, kind):
        self.place(which, kind).wait()
        for side in range(2):
            copy = self.hop(which, kind, self.me.half, self.me.core, side, True)
            copy.start()
            self.copies.append(copy)

    def forward(self, which, kind):
        other = 1 - self.me.half
        for side in range(2):
            self.hop(which, kind, other, self.me.core, side, True).wait_recv()
            copy = self.hop(which, kind, other, self.me.core, side, False)
            copy.start()
            self.copies.append(copy)

    def finish(self, which, kind):
        for side in range(2):
            self.hop(which, kind, 1 - self.me.half, 1 - self.me.core, side, False).wait_recv()

    def drain(self):
        for copy in self.copies:
            copy.wait_send()


SPAN = 38
BACK, FRONT = 14, 8


def word(i, j):
    start = (i * SPAN + j) * 8
    return pl.ds(start if isinstance(start, int) else pl.multiple_of(start, 8), 8)


def put_row(padded, row, first, values, halves=(0, 1)):
    for half in halves:
        i = row - 8 * half
        if 0 <= i < BACK:
            for group in range(4):
                padded[pl.ds((i * SPAN + first) * 8 + half * 4 + group, values.shape[0], stride=8), :] = (
                    values[:, group * 128 : group * 128 + 128]
                )


def rolled(values):
    return jnp.concatenate([values[4:], values[:4]], axis=0)


class Halo:
    def __init__(self, me, padded, tile, bufs):
        self.me, self.padded, self.tile = me, padded, tile
        self.rows, self.side_out, self.sides, self.corner_out, self.corners, self.sems = bufs
        self.copies = []
        self.row = (lax.div(me.x, 2) * 4 + me.y) * 2 + me.core

    def target(self, down, right):
        row = lax.rem(self.row + down + 16, 16)
        col = lax.rem(self.me.z + right + 4, 4)
        return {"row": row, "col": col, "dp": self.me.half}

    def messages(self):
        tile = self.tile
        yield tile.at[pl.ds(0, 96), :], self.rows.at[1], (-1, 0)
        yield tile.at[pl.ds(416, 96), :], self.rows.at[0], (1, 0)
        for side in range(2):
            yield self.side_out.at[side], self.sides.at[1 - side], (0, 2 * side - 1)
        for low in range(2):
            for side in range(2):
                yield (
                    self.corner_out.at[low, side],
                    self.corners.at[1 - low, 1 - side],
                    (2 * low - 1, 2 * side - 1),
                )

    def start(self):
        padded = self.padded
        for side, first in ((0, 3), (1, 32)):
            for j in range(3):
                lines = [padded[word(i, first + j), :] for i in range(3, 11)]
                self.side_out[side, j * 64 : j * 64 + 64, :] = jnp.concatenate(lines, 0).astype(BF)
            for low, top in ((0, 3), (1, 8)):
                lines = [
                    rolled(padded[word(top + i, first + j), :]) for i in range(3) for j in range(3)
                ]
                self.corner_out[low, side] = jnp.concatenate(lines + lines[:1], 0).astype(BF)
        for number, (src, dst, (down, right)) in enumerate(self.messages()):
            copy = remote(
                src, dst, self.sems.at[0, number], self.sems.at[1, number], self.target(down, right)
            )
            copy.start()
            self.copies.append(copy)

    def finish(self):
        padded = self.padded
        for number, (src, dst, _) in enumerate(self.messages()):
            remote(
                src, dst, self.sems.at[0, number], self.sems.at[1, number], self.target(1, 0)
            ).wait_recv()
        inside = [
            (self.row > 0).astype(F32),
            (self.row < 15).astype(F32),
        ]
        across = [
            (self.me.z > 0).astype(F32),
            (self.me.z < 3).astype(F32),
        ]
        for low in range(2):
            for r in range(3):
                values = self.rows[low, r * 32 : r * 32 + 32, :].astype(F32) * inside[low]
                put_row(padded, r + 19 * low, 3, values, (low,))
        for side, first in ((0, 0), (1, 35)):
            for j in range(3):
                lines = self.sides[side, j * 64 : j * 64 + 64, :].astype(F32) * across[side]
                for m in range(8):
                    line = lines[m * 8 : m * 8 + 8]
                    padded[word(m + 3, first + j), :] = line
                    at = first + j
                    if m >= 5:
                        padded[pl.ds(((m - 5) * SPAN + at) * 8 + 4, 4), :] = line[:4]
                    if m < 3:
                        padded[pl.ds(((m + 11) * SPAN + at) * 8, 4), :] = line[4:]
            for low in range(2):
                lines = self.corners[low, side].astype(F32) * (inside[low] * across[side])
                for i in range(3):
                    for j in range(3):
                        line = lines[(i * 3 + j) * 8 : (i * 3 + j) * 8 + 8]
                        start = ((i + 11 * low) * SPAN + first + j) * 8 + 4 * low
                        padded[pl.ds(start, 4), :] = line[4 * low : 4 * low + 4]

    def drain(self):
        for copy in self.copies:
            copy.wait_send()


def spread_taps(kernel, which, taps):
    for first in range(0, 56, 8):
        count = min(8, 49 - first)
        if count <= 0:
            break
        for group in range(4):
            values = kernel[which, first : first + count, group * 128 : group * 128 + 128]
            for half in range(2):
                if count == 8:
                    taps[pl.ds(first * 8 + half * 4 + group, 8, stride=8), :] = values
                else:
                    taps[pl.ds(first * 8 + half * 4 + group, 1), :] = values


def depthwise(padded, taps, result, flipped):
    def column(j, _):
        total = [None] * FRONT
        for q in range(7):
            values = [padded[word(i, j + q), :] for i in range(BACK)]
            for p in range(7):
                number = (6 - p) * 7 + 6 - q if flipped else p * 7 + q
                tap = taps[number * 8 : number * 8 + 8, :]
                for i in range(FRONT):
                    term = values[i + p] * tap
                    total[i] = term if total[i] is None else total[i] + term
        for i in range(FRONT):
            result[pl.ds(pl.multiple_of((i * 32 + j) * 8, 8), 8), :] = total[i]
        return 0

    lax.fori_loop(0, 32, column, 0)


def tap_grads(padded, upstream, small, base):
    for q in range(7):

        def column(j, totals):
            values = [padded[word(i, j + q), :] for i in range(BACK)]
            grads = [upstream[word(i + 3, j + 3), :] for i in range(FRONT)]
            result = []
            for p in range(7):
                total = totals[p]
                for i in range(FRONT):
                    total = total + values[i + p] * grads[i]
                result.append(total)
            return tuple(result)

        zero = jnp.zeros((8, 128), F32)
        totals = lax.fori_loop(0, 32, column, (zero,) * 7)
        for p in range(7):
            both = totals[p][:4] + totals[p][4:]
            for group in range(4):
                small[base + p * 7 + q : base + p * 7 + q + 1, group * 128 : group * 128 + 128] = both[
                    group : group + 1
                ]


def pixels(result, row):
    half, i = row // 8, row % 8
    return jnp.concatenate(
        [result[pl.ds(i * 256 + half * 4 + group, 32, stride=8), :] for group in range(4)], axis=1
    )


def dot(left, right, left_dim=1, right_dim=0):
    return lax.dot_general(
        left, right, (((left_dim,), (right_dim,)), ((), ())), preferred_element_type=F32
    )


def gelu_and_slope(values):
    square = values * values
    tangent = jnp.tanh(COEF * values * (1.0 + CUBIC * square))
    lift = 0.5 * (1.0 + tangent)
    slope = lift + 0.5 * values * (1.0 - tangent * tangent) * (COEF + (3.0 * COEF * CUBIC) * square)
    return values * lift, slope


CHUNK = 256


def step_kernel(
    slides, cotangent, kernel, channel, bias_in, shard_in, shard_out,
    output, grad_slides, final_in, final_out, final_small,
    full_in, full_out, padded0, padded1, padded_g, result, taps,
    normed, rstd, normal, turned, act, slope, hidden_grad, branch, carry, upstream, low,
    gm_tile, middle, grad_in, grad_out, small,
    *rest,
):
    me = Place()
    gather = Gather(me, shard_in, shard_out, full_in, full_out, rest[:5])
    padded = (padded0, padded1)
    tiles = (slides, middle)
    halos = [
        Halo(me, grid, tile, rest[5 + 6 * k : 11 + 6 * k])
        for k, (grid, tile) in enumerate(
            ((padded0, slides), (padded1, middle), (padded_g, gm_tile.at[1]), (padded_g, gm_tile.at[0]))
        )
    ]
    scratch = rest[30:]
    ways = {}
    for number, (kind, which) in enumerate(UNITS):
        bufs = scratch[number * 7 : number * 7 + 6]
        sems = scratch[number * 7 + 6]
        if kind is Small:
            ends = (small, final_small)
        elif kind is WeightIn:
            ends = (grad_in.at[which], final_in.at[which])
        else:
            ends = (grad_out.at[which], final_out.at[which])
        ways[kind, which] = Reduction(me, kind, *ends, bufs, sems)

    def reducing(which):
        return [ways[WeightOut, which], ways[WeightIn, which]]

    def line(which, number):
        return channel[which, number : number + 1, :]

    for which in range(2):
        for kind in range(2):
            gather.place(which, kind).start()

    def fill(grid, tile):
        for r in range(16):
            put_row(grid, r + 3, 3, tile[r * 32 : r * 32 + 32, :].astype(F32))

    fill(padded0, slides)
    partners = [me.along(axis, offset)[1] for axis in "xyz" for offset in (1, 2, 3)]
    around = [
        halos[0].target(down, right)
        for down in (-1, 0, 1)
        for right in (-1, 0, 1)
        if (down, right) != (0, 0)
    ]
    meet(partners + around + [me.sibling()])
    halos[0].start()
    gather.start(0, 0)
    gather.start(0, 1)
    gather.start(1, 0)
    for which in range(2):
        spread_taps(kernel, which, taps.at[which])
    small[...] = jnp.zeros_like(small)
    halos[0].finish()

    def normalise(which):
        depthwise(padded[which], taps.at[which], result, False)
        for r in range(16):
            rows = slice(r * 32, r * 32 + 32)
            mixed = pixels(result, r) + line(which, 0)
            center = mixed - jnp.mean(mixed, -1, keepdims=True)
            inverse = lax.rsqrt(jnp.mean(center * center, -1, keepdims=True) + EPSILON)
            values = center * inverse
            normed[which, rows, :] = values
            rstd[which, rows, :] = jnp.broadcast_to(inverse, (32, 128))
            normal[which, rows, :] = (values * line(which, 1) + line(which, 2)).astype(BF)

    def expand(which, with_grad):
        def chunk(c, _):
            cols = part(c * CHUNK, CHUNK)
            hidden = dot(normal[which], full_in[which, :, cols]) + bias_in[which : which + 1, cols]
            value, tilt = gelu_and_slope(hidden)
            act[which, :, cols] = value.astype(BF)
            if with_grad:
                grads = dot(low[...], full_out[which, cols, :], 1, 1) * tilt
                keep_hidden_grad(which, c, cols, grads)
            else:
                slope[:, cols] = tilt.astype(BF)
            return 0

        lax.fori_loop(0, 2048 // CHUNK, chunk, 0)

    def keep_hidden_grad(which, c, cols, grads):
        hidden_grad[:, cols] = grads.astype(BF)
        bias_grad[which : which + 1, cols] = jnp.sum(grads, 0, keepdims=True)

    bias_grad = rest[29]

    def contract(which):
        def chunk(n, _):
            cols = part(n * CHUNK, CHUNK)
            branch[which, :, cols] = (
                dot(act[which], full_out[which, :, cols]) + channel[which, 3:4, cols]
            )
            return 0

        lax.fori_loop(0, 512 // CHUNK, chunk, 0)

    def residual(which, into):
        for r in range(16):
            rows = slice(r * 32, r * 32 + 32)
            value = tiles[which][rows, :].astype(F32) + line(which, 4) * branch[which, rows, :]
            into[rows, :] = value.astype(BF)

    def enter(which, read):
        for r in range(16):
            rows = slice(r * 32, r * 32 + 32)
            grads = read(rows) * line(which, 4)
            low[rows, :] = grads.astype(BF)
            add_rows(0, grads)

    def add_rows(slot, values):
        total = values[0:8] + values[8:16] + (values[16:24] + values[24:32])
        carry[slot] = carry[slot] + total

    def weight_grads(which):
        def chunk(c, _):
            cols = part(c * CHUNK, CHUNK)
            grad_out[which, cols, :] = dot(act[which, :, cols], low[...], 0, 0).astype(BF)
            grad_in[which, :, cols] = dot(turned[...], hidden_grad[:, cols]).astype(BF)
            return 0

        turned[...] = normal[which].T
        lax.fori_loop(0, 2048 // CHUNK, chunk, 0)

    def normal_grads(which, target):
        def chunk(n, _):
            rows = part(n * CHUNK, CHUNK)
            target[:, rows] = dot(hidden_grad[...], full_in[which, rows, :], 1, 1)
            return 0

        lax.fori_loop(0, 512 // CHUNK, chunk, 0)

    def leave(which, grads_ref):
        for r in range(16):
            rows = slice(r * 32, r * 32 + 32)
            grads = grads_ref[rows, :]
            values = normed[which, rows, :]
            add_rows(2, grads)
            add_rows(1, grads * values)
            scaled = grads * line(which, 1)
            mean = jnp.mean(scaled, -1, keepdims=True)
            tilt = jnp.mean(scaled * values, -1, keepdims=True)
            mixed = (scaled - mean - values * tilt) * rstd[which, rows, 0:1]
            add_rows(3, mixed)
            put_row(padded_g, r + 3, 3, mixed)
            gm_tile[which, rows, :] = mixed.astype(BF)

    def scale_grad(which, read):
        for r in range(16):
            rows = slice(r * 32, r * 32 + 32)
            add_rows(4, read(rows) * branch[which, rows, :])

    def settle(which):
        for slot, row in ((3, 0), (1, 1), (2, 2), (0, 3), (4, 4)):
            at = which * 64 + 49 + row
            small[at : at + 1, :] = jnp.sum(carry[slot], 0, keepdims=True)
        for c in range(4):
            at = which * 64 + 54 + c
            small[at : at + 1, :] = bias_grad[which : which + 1, c * 512 : c * 512 + 512]

    def from_cotangent(rows):
        return cotangent[rows, :].astype(F32)

    def from_upstream(rows):
        return upstream[rows, :]

    gather.forward(0, 0)
    normalise(0)
    gather.finish(0, 0)
    expand(0, False)
    gather.forward(0, 1)
    gather.finish(0, 1)
    contract(0)
    residual(0, middle)
    fill(padded1, middle)
    halos[1].start()
    gather.start(1, 1)
    gather.forward(1, 0)
    carry[...] = jnp.zeros_like(carry)
    enter(1, from_cotangent)
    halos[1].finish()
    normalise(1)
    gather.finish(1, 0)
    gather.forward(1, 1)
    gather.finish(1, 1)
    expand(1, True)
    normal_grads(1, upstream)
    leave(1, upstream)
    halos[2].start()
    weight_grads(1)
    for way in reducing(1):
        way.core_start()
    contract(1)
    residual(1, output)
    scale_grad(1, from_cotangent)
    settle(1)
    for way in reducing(1):
        way.core_finish()
        way.split_start(0)
    tap_grads(padded1, padded_g, small, 64)
    halos[2].finish()
    depthwise(padded_g, taps.at[1], result, True)
    for r in range(16):
        rows = slice(r * 32, r * 32 + 32)
        upstream[rows, :] = from_cotangent(rows) + pixels(result, r)
    for way in reducing(1):
        way.split_finish(0)
        way.split_start(1)
    carry[...] = jnp.zeros_like(carry)
    enter(0, from_upstream)
    scale_grad(0, from_upstream)

    def chunk(c, _):
        cols = part(c * CHUNK, CHUNK)
        grads = dot(low[...], full_out[0, cols, :], 1, 1) * slope[:, cols].astype(F32)
        keep_hidden_grad(0, c, cols, grads)
        return 0

    lax.fori_loop(0, 2048 // CHUNK, chunk, 0)
    for way in reducing(1):
        way.split_finish(1)
        way.across_start()
    weight_grads(0)
    for way in reducing(0):
        way.core_start()
    normal_grads(0, branch.at[1])
    for way in reducing(1):
        way.across_finish()
        way.join_start(1)
    for way in reducing(0):
        way.core_finish()
        way.split_start(0)
    leave(0, branch.at[1])
    halos[3].start()
    settle(0)
    for way in reducing(1):
        way.join_finish(1)
        way.join_start(0)
    tap_grads(padded0, padded_g, small, 0)
    ways[Small, None].core_start()
    halos[3].finish()
    depthwise(padded_g, taps.at[0], result, True)
    for r in range(16):
        rows = slice(r * 32, r * 32 + 32)
        grad_slides[rows, :] = (upstream[rows, :] + pixels(result, r)).astype(BF)
    for way in reducing(1):
        way.join_finish(0)
        way.share_start()
    last = [ways[Small, None]] + reducing(0)
    last[0].core_finish()
    last[0].split_start(0)
    for way in last:
        way.split_finish(0)
        way.split_start(1)
    for way in last:
        way.split_finish(1)
        way.across_start()
    for way in last:
        way.across_finish()
        way.join_start(1)
    for way in last:
        way.join_finish(1)
        way.join_start(0)
    for way in last:
        way.join_finish(0)
        way.share_start()
    for way in reducing(1) + last:
        way.share_finish()
    for way in reducing(1) + last + halos + [gather]:
        way.drain()


def halo_scratch():
    return [
        pltpu.VMEM((2, 96, 512), BF),
        pltpu.VMEM((2, 192, 128), BF),
        pltpu.VMEM((2, 192, 128), BF),
        pltpu.VMEM((2, 2, 80, 128), BF),
        pltpu.VMEM((2, 2, 80, 128), BF),
        pltpu.SemaphoreType.DMA((2, 8)),
    ]


def whole_step(slides, cotangent, kernel, channel, bias_in, weight_in, weight_out):
    vmem = pl.BlockSpec(memory_space=pltpu.VMEM)
    grid = pltpu.VMEM((BACK * SPAN * 8, 128), F32)
    scratch = [
        pltpu.VMEM((2, 512, 2048), BF),
        pltpu.VMEM((2, 2048, 512), BF),
        grid,
        grid,
        grid,
        pltpu.VMEM((8 * 32 * 8, 128), F32),
        pltpu.VMEM((2, 49 * 8, 128), F32),
        pltpu.VMEM((2, 512, 512), F32),
        pltpu.VMEM((2, 512, 128), F32),
        pltpu.VMEM((2, 512, 512), BF),
        pltpu.VMEM((512, 512), BF),
        pltpu.VMEM((2, 512, 2048), BF),
        pltpu.VMEM((512, 2048), BF),
        pltpu.VMEM((512, 2048), BF),
        pltpu.VMEM((2, 512, 512), F32),
        pltpu.VMEM((5, 8, 512), F32),
        pltpu.VMEM((512, 512), F32),
        pltpu.VMEM((512, 512), BF),
        pltpu.VMEM((2, 512, 512), BF),
        pltpu.VMEM((512, 512), BF),
        pltpu.VMEM((2, 512, 2048), BF),
        pltpu.VMEM((2, 2048, 512), BF),
        pltpu.VMEM((128, 512), F32),
    ]
    scratch += [pltpu.SemaphoreType.DMA((2, 2))]
    scratch += [pltpu.SemaphoreType.DMA((2, 2, 2)) for _ in range(4)]
    for _ in range(4):
        scratch += halo_scratch()
    extra = [pltpu.VMEM((2, 2048), F32)]
    reductions = sum([reduction_scratch(kind) for kind, _ in UNITS], [])
    return pl.pallas_call(
        step_kernel,
        out_shape=(
            jax.ShapeDtypeStruct((512, 512), BF),
            jax.ShapeDtypeStruct((512, 512), BF),
            jax.ShapeDtypeStruct((2, 256, 2048), BF),
            jax.ShapeDtypeStruct((2, 2048, 256), BF),
            jax.ShapeDtypeStruct((128, 512), F32),
        ),
        in_specs=[vmem] * 5 + [pl.BlockSpec(memory_space=pl.ANY)] * 2,
        out_specs=[vmem] * 5,
        scratch_shapes=scratch + extra + reductions,
        compiler_params=pltpu.CompilerParams(
            collective_id=0, has_side_effects=True, vmem_limit_bytes=67043328
        ),
        name="whole_step",
    )(slides, cotangent, kernel, channel, bias_in, weight_in, weight_out)


def per_device(
    slides,
    cotangent,
    kernel,
    kernel_bias,
    norm_gain,
    norm_bias,
    weight_in,
    bias_in,
    weight_out,
    bias_out,
    layer_scale,
):
    channels = slides.shape[-1]
    channel = jnp.stack([kernel_bias, norm_gain, norm_bias, bias_out, layer_scale], axis=1)
    output, grad_slides, total_in, total_out, small = whole_step(
        slides.reshape(-1, channels),
        cotangent.reshape(-1, channels),
        kernel.reshape(2, 49, channels),
        channel,
        bias_in,
        weight_in,
        weight_out,
    )
    small = small.reshape(2, 64, channels)
    return (
        output.reshape(slides.shape),
        grad_slides.reshape(slides.shape),
        total_in.astype(F32),
        total_out.astype(F32),
        small[:, :49].reshape(2, 7, 7, channels),
        small[:, 49:54],
        small[:, 54:58].reshape(2, 4 * channels),
    )


def solution(mesh):
    whole = P("dp", "row", "col", None)
    return jax.shard_map(
        per_device,
        mesh=mesh,
        in_specs=(whole, whole) + (P(),) * 4 + (P(None, "dp", None), P(), P(None, None, "dp"), P(), P()),
        out_specs=(whole, whole, P(None, "dp", None), P(None, None, "dp"), P(), P(), P()),
        check_vma=False,
    )
```

time: 657 us -> 164 us (0.25); the launches traced: 647 us -> 164 us
  waiting for transfers between devices: 229 us -> 0 us
  Pallas kernels: 0 us -> 144 us
  starting transfers between devices: 123 us -> 0 us
  other arithmetic: 115 us -> 6.62 us
  blocking collectives: 70.8 us -> 0 us
  matrix products: 42.8 us -> 0 us
  local copies, waits for them, and re-layouts: 49.2 us -> 12 us
  between operations: 17.6 us -> 0.65 us
    pallas_call x0 -> x1, Pallas kernels: none -> 144 us  [whole_step(): pl.pallas_call(step_kernel, out_shape=(jax.ShapeDtypeStruct((512, 512), B...]
    all_to_all x12 -> x0, waiting for transfers between devices: 102 us -> none  [the longest x8 72.5 us: sent_and_summed(): pieces = lax.all_to_all(cut_along(shard, dim, size), axis, 0, 0, tiled=True)]
    reduce_sum x24 -> x0, other arithmetic: 83 us -> none  [the longest x9 29.3 us: tap_grads(): line.append(jnp.sum(window * upstream, axis=(0, 1, 2)))]
    all_to_all x12 -> x0, starting transfers between devices: 77.2 us -> none  [the longest x8 53.7 us: sent_and_summed(): pieces = lax.all_to_all(cut_along(shard, dim, size), axis, 0, 0, tiled=True)]
    psum x1 -> x0, waiting for transfers between devices: 70.9 us -> none  [per_device(): lax.psum((local_taps, channel_grads, grad_bias), ('row', 'col', 'dp'))]
    psum x1 -> x0, blocking collectives: 70.8 us -> none  [per_device(): lax.psum((local_taps, channel_grads, grad_bias), ('row', 'col', 'dp'))]
    all_gather x2 -> x0, waiting for transfers between devices: 49.1 us -> none  [turned_gather(): result = lax.all_gather(both, axis, axis=0, tiled=True)]
    ppermute x16 -> x0, starting transfers between devices: 45.3 us -> none  [the longest x8 29.9 us: with_halo(): lax.ppermute(lax.slice_in_dim(block, block.shape[dim] - width, None, axis...]
  transfers between devices with their start and end apart: 31 -> 0, of which waited for: 18 -> 0; matrix products, arithmetic and copies ran while one was open for 27% -> 0% of each run, Pallas kernels for 0% -> 0%
where the time goes in v1:
time: 164 us
  Pallas kernels  144 us (88%)
  local copies, waits for them, and re-layouts  12 us (7%)
  other arithmetic  6.62 us (4%)
    pallas_call x1, Pallas kernels, whole_step(): pl.pallas_call(step_kernel, out_shape=(jax.ShapeDtypeStruct((512, 512), B...  144 us
    convert_element_type x1, other arithmetic, per_device(): total_in.astype(F32)  4.28 us
    another operation x6, local copies, waits for them, and re-layouts, per_device(): jnp.stack([kernel_bias, norm_gain, norm_bias, bias_out, layer_scale], axi...  4.1 us
    unnamed x11, local copies, waits for them, and re-layouts  3.69 us

profile of v1, /device:TPU:1, one launch (start us, length us, event | category | flops | bytes accessed | tf_op | source)
XLA Modules:
  0.0 163.6 jit_solution(6417952925825760765)
XLA Ops:
  0.6 0.7 stack.18
  1.3 0.7 stack.19
  2.0 0.7 stack.20
  2.7 0.7 stack.21
  3.4 0.7 stack.22
  4.1 0.6 stack.23.channel
  4.7 1.7 %copy.21.kernel = f32[2,49,512]{2,1,0:T(8,128)} copy(f32[2,49,512]{2,0,1:T(2,128)} %bitcast.17) | data formatting | bytes 401408 | tf_op jit(solution)/shard_map/reshape | solution.py:885
  6.4 144.4 %whole_step.1 = (bf16[512,512]{1,0:T(8,128)(2,1)}, bf16[512,512]{1,0:T(8,128)(2,1)}, bf16[2,256,2048]{2,1,0:T(8,128)(2,1)}, bf16[2,2048,256]{2,1,0:T(8,128)(2,1)}, f32[128,512]{1,0:T(8,128)}) custom-call(bf16[512,512]{1,0:T(8,128)(2,1)} %bitcast.12, bf16[512,512]{1,0:T(8,128)(2,1)} %bitcast.13, f32[2,49,512]{2,1,0:T(8,128)} %copy.21.kernel, ...), custom_call_target="tpu_custom_call" | custom-call | tf_op jit(solution)/shard_map/whole_step/pallas_call | solution.py:848
  150.8 0.9 slice_bitcast_fusion
  151.6 0.6 copy.25
  152.2 0.8 slice.13
  153.0 1.0 slice.12
  154.0 0.8 copy.22
  154.8 0.6 copy.24
  155.4 0.0 copy-start
  155.4 4.3 %convert_element_type.6 = f32[2,256,2048]{2,1,0:T(8,128)} convert(bf16[2,256,2048]{2,1,0:T(8,128)(2,1)} %get-tuple-element.14) | non-fusion elementwise | flops 1048576 | bytes 6291456 | tf_op jit(solution)/shard_map/convert_element_type | solution.py:895
  159.7 0.0 copy-done
  159.7 0.0 copy-start.2
  159.7 0.0 copy-start.1
  159.7 2.3 %convert_element_type.7 = f32[2,2048,256]{2,1,0:T(8,128)} convert(bf16[2,2048,256]{2,1,0:T(8,128)(2,1)S(1)} %copy-done) | non-fusion elementwise | flops 1048576 | bytes 6291456 | tf_op jit(solution)/shard_map/convert_element_type | solution.py:896
  162.1 0.0 copy-done.2
  162.1 0.8 copy.28
  162.8 0.0 copy-done.1
  162.9 0.8 copy.29
Async XLA Ops:
  155.4 4.3 %copy-start = (bf16[2,2048,256]{2,1,0:T(8,128)(2,1)S(1)}, bf16[2,2048,256]{2,1,0:T(8,128)(2,1)}, u32[]{:S(2)}) copy-start(bf16[2,2048,256]{2,1,0:T(8,128)(2,1)} %get-tuple-element.15) | copy-start | bytes 6291460
  159.7 2.4 %copy-start.2 = (bf16[512,512]{1,0:T(8,128)(2,1)S(1)}, bf16[512,512]{1,0:T(8,128)(2,1)}, u32[]{:S(2)}) copy-start(bf16[512,512]{1,0:T(8,128)(2,1)} %get-tuple-element.12) | copy-start | bytes 1572868
  159.7 3.1 %copy-start.1 = (bf16[512,512]{1,0:T(8,128)(2,1)S(1)}, bf16[512,512]{1,0:T(8,128)(2,1)}, u32[]{:S(2)}) copy-start(bf16[512,512]{1,0:T(8,128)(2,1)} %get-tuple-element.13) | copy-start | bytes 1572868

commit v2 on v1

--- a/solution.py
+++ b/solution.py
@@ -63,16 +63,17 @@
 
 
 class WeightIn:
-    received = (2, 128, 2048)
-    first = (2, 64, 512)
-    second = (2, 64, 128)
+    received = (128, 2048)
+    turn = (64, 2048)
+    first = (64, 512)
+    second = (64, 128)
     third = (64, 128)
 
     def offered(grad, half, core):
         return grad.at[part(half * 256 + core * 128, 128), :]
 
-    def cut(got, turn, index):
-        return got.at[:, turn * 64 : turn * 64 + 64, part(index * 512, 512)]
+    def cut(got, halves, turn, index):
+        return got.at[halves, turn * 64 : turn * 64 + 64, part(index * 512, 512)]
 
     def cut_again(block, index):
         return block.at[:, :, part(index * 128, 128)]
@@ -88,16 +89,17 @@
 
 
 class WeightOut:
-    received = (2, 2048, 128)
-    first = (2, 256, 128)
-    second = (2, 64, 128)
+    received = (2048, 128)
+    turn = (1024, 128)
+    first = (256, 128)
+    second = (64, 128)
     third = (64, 128)
 
     def offered(grad, half, core):
         return grad.at[:, part(half * 256 + core * 128, 128)]
 
-    def cut(got, turn, index):
-        return got.at[:, part(turn * 1024 + index * 256, 256), :]
+    def cut(got, halves, turn, index):
+        return got.at[halves, part(turn * 1024 + index * 256, 256), :]
 
     def cut_again(block, index):
         return block.at[:, part(index * 64, 64), :]
@@ -113,16 +115,17 @@
 
 
 class Small:
-    received = (1, 64, 512)
-    first = (1, 32, 128)
-    second = (1, 8, 128)
+    received = (64, 512)
+    turn = (32, 512)
+    first = (32, 128)
+    second = (8, 128)
     third = (8, 128)
 
     def offered(grad, half, core):
         return grad.at[part(core * 64, 64), :]
 
-    def cut(got, turn, index):
-        return got.at[:, turn * 32 : turn * 32 + 32, part(index * 128, 128)]
+    def cut(got, halves, turn, index):
+        return got.at[halves, turn * 32 : turn * 32 + 32, part(index * 128, 128)]
 
     def cut_again(block, index):
         return block.at[:, part(index * 8, 8), :]
@@ -138,15 +141,34 @@
 
 
 class Reduction:
-    def __init__(self, me, kind, grad, final, bufs, sems):
-        self.me, self.kind, self.grad, self.final = me, kind, grad, final
-        self.got, self.r1, self.b1, self.r2, self.b2, self.r3 = bufs
+    def __init__(self, me, kind, early, grad, final, bufs, sems):
+        self.me, self.kind, self.early, self.grad, self.final = me, kind, early, grad, final
+        self.got, self.given, self.r1, self.b1, self.r2, self.b2, self.r3 = bufs
         self.sems = sems
         self.halves = 1 if kind is Small else 2
         self.copies = []
+        self.steps = [
+            [self.core_start],
+            [self.core_finish, lambda: self.split_start(0)],
+            [lambda: self.split_finish(0), lambda: self.split_start(1)],
+            [lambda: self.split_finish(1), self.across_start],
+            [self.across_finish, lambda: self.join_start(1)],
+            [lambda: self.join_finish(1), lambda: self.join_start(0)],
+            [lambda: self.join_finish(0), self.share_start],
+            [self.share_finish],
+        ]
+        if early:
+            self.steps[1:2] = [
+                [self.core_finish, self.give_start],
+                [self.give_finish, lambda: self.split_start(0)],
+            ]
+
+    def advance(self):
+        for action in self.steps.pop(0):
+            action()
 
     def sem(self, way, turn, step, slot):
-        return self.sems.at[way, (turn * 7 + step) * 4 + slot]
+        return self.sems.at[way, (turn * 8 + step) * 4 + slot]
 
     def go(self, src, dst, turn, step, send_slot, recv_slot, target):
         copy = remote(
@@ -174,7 +196,8 @@
 
     def block(self, turn, step, index):
         if step == 0:
-            return self.kind.cut(self.got, turn, index)
+            halves = pl.ds(self.me.half, 1) if self.early else slice(None)
+            return self.kind.cut(self.got, halves, turn, index)
         return self.kind.cut_again(self.b1.at[turn], index)
 
     def split_start(self, step):
@@ -202,9 +225,30 @@
                 total = total + target[turn, offset - 1].astype(F32)
             result[turn] = total.astype(result.dtype)
 
+    def turn_rows(self, half, turn):
+        size = self.kind.turn[0]
+        return self.got.at[half, turn * size : turn * size + size, :]
+
+    def give_start(self):
+        for turn, offset in ((0, 1), (1, 3)):
+            _, device = self.me.along("x", offset)
+            src = self.turn_rows(1 - self.me.half, turn)
+            self.go(src, self.given.at[turn], turn, 7, 0, 0, device)
+
+    def give_finish(self):
+        for turn in range(2):
+            self.landed(self.given.at[turn], turn, 7, 0)
+            own = self.turn_rows(self.me.half, turn)
+            total = own[...].astype(F32) + self.given[turn].astype(F32)
+            own[...] = total.astype(self.got.dtype)
+
     def across_start(self):
         for turn in range(2):
             block = self.b2.at[turn]
+            if self.early:
+                _, device = self.me.along("x", 2)
+                self.go(block.at[0], self.r3.at[turn, 0], turn, 3, 0, 0, device)
+                continue
             for offset in (1, 3, 2):
                 index, device = self.me.along("x", offset)
                 src = block.at[lax.rem(index, 2) if self.halves == 2 else 0]
@@ -214,12 +258,16 @@
     def across_finish(self):
         me = self.me
         for turn in range(2):
-            for offset in (1, 3, 2):
-                index, _ = me.along("x", offset)
-                self.landed(self.r3.at[turn, index], turn, 3, index)
-            total = self.r3[turn, 0].astype(F32)
-            for index in range(1, 4):
-                total = total + self.r3[turn, index].astype(F32)
+            if self.early:
+                self.landed(self.r3.at[turn, 0], turn, 3, 0)
+                total = self.b2[turn, 0].astype(F32) + self.r3[turn, 0].astype(F32)
+            else:
+                for offset in (1, 3, 2):
+                    index, _ = me.along("x", offset)
+                    self.landed(self.r3.at[turn, index], turn, 3, index)
+                total = self.r3[turn, 0].astype(F32)
+                for index in range(1, 4):
+                    total = total + self.r3[turn, index].astype(F32)
             one, two = (getattr(me, axis) for axis in ORDERS[turn])
             block = self.kind.placed(self.final, me.core, turn, one, two)
             block[...] = total.astype(self.final.dtype)
@@ -261,20 +309,28 @@
             copy.wait_send()
 
 
-def reduction_scratch(kind):
+def reduction_scratch(kind, early):
     dtype = F32 if kind is Small else BF
+    halves = 1 if kind is Small or early else 2
     return [
-        pltpu.VMEM(kind.received, dtype),
-        pltpu.VMEM((2, 3, *kind.first), dtype),
-        pltpu.VMEM((2, *kind.first), dtype),
-        pltpu.VMEM((2, 3, *kind.second), dtype),
-        pltpu.VMEM((2, *kind.second), dtype),
+        pltpu.VMEM((1 if kind is Small else 2, *kind.received), dtype),
+        pltpu.VMEM((2, *kind.turn) if early else (2, 8, 128), dtype),
+        pltpu.VMEM((2, 3, halves, *kind.first), dtype),
+        pltpu.VMEM((2, halves, *kind.first), dtype),
+        pltpu.VMEM((2, 3, halves, *kind.second), dtype),
+        pltpu.VMEM((2, halves, *kind.second), dtype),
         pltpu.VMEM((2, 4, *kind.third), dtype),
-        pltpu.SemaphoreType.DMA((2, 56)),
+        pltpu.SemaphoreType.DMA((2, 64)),
     ]
 
 
-UNITS = ((Small, None), (WeightOut, 1), (WeightIn, 1), (WeightOut, 0), (WeightIn, 0))
+UNITS = (
+    (Small, None, False),
+    (WeightOut, 1, True),
+    (WeightIn, 1, True),
+    (WeightOut, 0, False),
+    (WeightIn, 0, True),
+)
 
 
 class Gather:
@@ -440,20 +496,14 @@
 
 
 def spread_taps(kernel, which, taps):
-    for first in range(0, 56, 8):
-        count = min(8, 49 - first)
-        if count <= 0:
-            break
+    for p in range(7):
         for group in range(4):
-            values = kernel[which, first : first + count, group * 128 : group * 128 + 128]
+            values = kernel[p, :, which, group * 128 : group * 128 + 128]
             for half in range(2):
-                if count == 8:
-                    taps[pl.ds(first * 8 + half * 4 + group, 8, stride=8), :] = values
-                else:
-                    taps[pl.ds(first * 8 + half * 4 + group, 1), :] = values
-
-
-def depthwise(padded, taps, result, flipped):
+                taps[pl.ds(p * 56 + half * 4 + group, 7, stride=8), :] = values
+
+
+def depthwise(padded, taps, result, flipped, first=0, last=32):
     def column(j, _):
         total = [None] * FRONT
         for q in range(7):
@@ -468,11 +518,11 @@
             result[pl.ds(pl.multiple_of((i * 32 + j) * 8, 8), 8), :] = total[i]
         return 0
 
-    lax.fori_loop(0, 32, column, 0)
-
-
-def tap_grads(padded, upstream, small, base):
-    for q in range(7):
+    lax.fori_loop(first, last, column, 0)
+
+
+def tap_grads(padded, upstream, small, base, columns):
+    for q in columns:
 
         def column(j, totals):
             values = [padded[word(i, j + q), :] for i in range(BACK)]
@@ -520,9 +570,10 @@
 
 
 def step_kernel(
-    slides, cotangent, kernel, channel, bias_in, shard_in, shard_out,
+    slides, cotangent, kernel, kernel_bias, norm_gain, norm_bias, bias_out, layer_scale, bias_in,
+    shard_in, shard_out,
     output, grad_slides, final_in, final_out, final_small,
-    full_in, full_out, padded0, padded1, padded_g, result, taps,
+    full_in, full_out, padded0, padded1, padded_g0, padded_g1, result, taps,
     normed, rstd, normal, turned, act, slope, hidden_grad, branch, carry, upstream, low,
     gm_tile, middle, grad_in, grad_out, small,
     *rest,
@@ -530,71 +581,76 @@
     me = Place()
     gather = Gather(me, shard_in, shard_out, full_in, full_out, rest[:5])
     padded = (padded0, padded1)
+    padded_g = (padded_g0, padded_g1)
     tiles = (slides, middle)
     halos = [
         Halo(me, grid, tile, rest[5 + 6 * k : 11 + 6 * k])
         for k, (grid, tile) in enumerate(
-            ((padded0, slides), (padded1, middle), (padded_g, gm_tile.at[1]), (padded_g, gm_tile.at[0]))
+            ((padded0, slides), (padded1, middle), (padded_g1, gm_tile.at[1]), (padded_g0, gm_tile.at[0]))
         )
     ]
     scratch = rest[30:]
     ways = {}
-    for number, (kind, which) in enumerate(UNITS):
-        bufs = scratch[number * 7 : number * 7 + 6]
-        sems = scratch[number * 7 + 6]
+    for number, (kind, which, early) in enumerate(UNITS):
+        bufs = scratch[number * 8 : number * 8 + 7]
+        sems = scratch[number * 8 + 7]
         if kind is Small:
             ends = (small, final_small)
         elif kind is WeightIn:
             ends = (grad_in.at[which], final_in.at[which])
         else:
             ends = (grad_out.at[which], final_out.at[which])
-        ways[kind, which] = Reduction(me, kind, *ends, bufs, sems)
+        ways[kind, which] = Reduction(me, kind, early, *ends, bufs, sems)
 
     def reducing(which):
         return [ways[WeightOut, which], ways[WeightIn, which]]
 
-    def line(which, number):
-        return channel[which, number : number + 1, :]
+    def line(which, ref):
+        return ref[which : which + 1, :]
 
     for which in range(2):
         for kind in range(2):
             gather.place(which, kind).start()
 
+    scope = jax.named_scope
+
     def fill(grid, tile):
         for r in range(16):
             put_row(grid, r + 3, 3, tile[r * 32 : r * 32 + 32, :].astype(F32))
 
-    fill(padded0, slides)
     partners = [me.along(axis, offset)[1] for axis in "xyz" for offset in (1, 2, 3)]
     around = [
-        halos[0].target(down, right)
-        for down in (-1, 0, 1)
-        for right in (-1, 0, 1)
-        if (down, right) != (0, 0)
+        halos[0].target(down, right) for down in (-1, 0, 1) for right in (-1, 0, 1) if down
     ]
-    meet(partners + around + [me.sibling()])
-    halos[0].start()
-    gather.start(0, 0)
-    gather.start(0, 1)
-    gather.start(1, 0)
-    for which in range(2):
-        spread_taps(kernel, which, taps.at[which])
-    small[...] = jnp.zeros_like(small)
-    halos[0].finish()
+    with scope("p00a_fill"):
+        fill(padded0, slides)
+        for which in range(2):
+            spread_taps(kernel, which, taps.at[which])
+        small[...] = jnp.zeros_like(small)
+        carry[...] = jnp.zeros_like(carry)
+    with scope("p00b_meet"):
+        meet(partners + around + [me.sibling()])
+    with scope("p00c_start"):
+        halos[0].start()
+        gather.start(0, 0)
+        gather.start(0, 1)
+        gather.start(1, 0)
+
+    def filter_map(which, first, last):
+        depthwise(padded[which], taps.at[which], result, False, first, last)
 
     def normalise(which):
-        depthwise(padded[which], taps.at[which], result, False)
         for r in range(16):
             rows = slice(r * 32, r * 32 + 32)
-            mixed = pixels(result, r) + line(which, 0)
+            mixed = pixels(result, r) + line(which, kernel_bias)
             center = mixed - jnp.mean(mixed, -1, keepdims=True)
             inverse = lax.rsqrt(jnp.mean(center * center, -1, keepdims=True) + EPSILON)
             values = center * inverse
             normed[which, rows, :] = values
             rstd[which, rows, :] = jnp.broadcast_to(inverse, (32, 128))
-            normal[which, rows, :] = (values * line(which, 1) + line(which, 2)).astype(BF)
-
-    def expand(which, with_grad):
+            normal[which, rows, :] = (values * line(which, norm_gain) + line(which, norm_bias)).astype(BF)
+
+    def expand(which, with_grad, first=0, last=2048 // CHUNK):
         def chunk(c, _):
             cols = part(c * CHUNK, CHUNK)
             hidden = dot(normal[which], full_in[which, :, cols]) + bias_in[which : which + 1, cols]
@@ -607,7 +663,7 @@
                 slope[:, cols] = tilt.astype(BF)
             return 0
 
-        lax.fori_loop(0, 2048 // CHUNK, chunk, 0)
+        lax.fori_loop(first, last, chunk, 0)
 
     def keep_hidden_grad(which, c, cols, grads):
         hidden_grad[:, cols] = grads.astype(BF)
@@ -619,7 +675,7 @@
         def chunk(n, _):
             cols = part(n * CHUNK, CHUNK)
             branch[which, :, cols] = (
-                dot(act[which], full_out[which, :, cols]) + channel[which, 3:4, cols]
+                dot(act[which], full_out[which, :, cols]) + bias_out[which : which + 1, cols]
             )
             return 0
 
@@ -628,19 +684,19 @@
     def residual(which, into):
         for r in range(16):
             rows = slice(r * 32, r * 32 + 32)
-            value = tiles[which][rows, :].astype(F32) + line(which, 4) * branch[which, rows, :]
+            value = tiles[which][rows, :].astype(F32) + line(which, layer_scale) * branch[which, rows, :]
             into[rows, :] = value.astype(BF)
 
     def enter(which, read):
         for r in range(16):
             rows = slice(r * 32, r * 32 + 32)
-            grads = read(rows) * line(which, 4)
+            grads = read(rows) * line(which, layer_scale)
             low[rows, :] = grads.astype(BF)
-            add_rows(0, grads)
-
-    def add_rows(slot, values):
+            add_rows(which, 0, grads)
+
+    def add_rows(which, slot, values):
         total = values[0:8] + values[8:16] + (values[16:24] + values[24:32])
-        carry[slot] = carry[slot] + total
+        carry[which, slot] = carry[which, slot] + total
 
     def weight_grads(which):
         def chunk(c, _):
@@ -665,25 +721,25 @@
             rows = slice(r * 32, r * 32 + 32)
             grads = grads_ref[rows, :]
             values = normed[which, rows, :]
-            add_rows(2, grads)
-            add_rows(1, grads * values)
-            scaled = grads * line(which, 1)
+            add_rows(which, 2, grads)
+            add_rows(which, 1, grads * values)
+            scaled = grads * line(which, norm_gain)
             mean = jnp.mean(scaled, -1, keepdims=True)
             tilt = jnp.mean(scaled * values, -1, keepdims=True)
             mixed = (scaled - mean - values * tilt) * rstd[which, rows, 0:1]
-            add_rows(3, mixed)
-            put_row(padded_g, r + 3, 3, mixed)
+            add_rows(which, 3, mixed)
+            put_row(padded_g[which], r + 3, 3, mixed)
             gm_tile[which, rows, :] = mixed.astype(BF)
 
     def scale_grad(which, read):
         for r in range(16):
             rows = slice(r * 32, r * 32 + 32)
-            add_rows(4, read(rows) * branch[which, rows, :])
+            add_rows(which, 4, read(rows) * branch[which, rows, :])
 
     def settle(which):
         for slot, row in ((3, 0), (1, 1), (2, 2), (0, 3), (4, 4)):
             at = which * 64 + 49 + row
-            small[at : at + 1, :] = jnp.sum(carry[slot], 0, keepdims=True)
+            small[at : at + 1, :] = jnp.sum(carry[which, slot], 0, keepdims=True)
         for c in range(4):
             at = which * 64 + 54 + c
             small[at : at + 1, :] = bias_grad[which : which + 1, c * 512 : c * 512 + 512]
@@ -694,51 +750,75 @@
     def from_upstream(rows):
         return upstream[rows, :]
 
-    gather.forward(0, 0)
-    normalise(0)
-    gather.finish(0, 0)
-    expand(0, False)
-    gather.forward(0, 1)
-    gather.finish(0, 1)
-    contract(0)
-    residual(0, middle)
-    fill(padded1, middle)
-    halos[1].start()
-    gather.start(1, 1)
-    gather.forward(1, 0)
-    carry[...] = jnp.zeros_like(carry)
-    enter(1, from_cotangent)
-    halos[1].finish()
-    normalise(1)
-    gather.finish(1, 0)
-    gather.forward(1, 1)
-    gather.finish(1, 1)
-    expand(1, True)
-    normal_grads(1, upstream)
-    leave(1, upstream)
-    halos[2].start()
-    weight_grads(1)
-    for way in reducing(1):
-        way.core_start()
-    contract(1)
-    residual(1, output)
-    scale_grad(1, from_cotangent)
-    settle(1)
-    for way in reducing(1):
-        way.core_finish()
-        way.split_start(0)
-    tap_grads(padded1, padded_g, small, 64)
-    halos[2].finish()
-    depthwise(padded_g, taps.at[1], result, True)
-    for r in range(16):
-        rows = slice(r * 32, r * 32 + 32)
-        upstream[rows, :] = from_cotangent(rows) + pixels(result, r)
-    for way in reducing(1):
-        way.split_finish(0)
-        way.split_start(1)
-    carry[...] = jnp.zeros_like(carry)
-    enter(0, from_upstream)
-    scale_grad(0, from_upstream)
+    with scope("p00e_halo0"):
+        enter(1, from_cotangent)
+        halos[0].finish()
+    with scope("p01_depth0"):
+        filter_map(0, 0, 20)
+    with scope("p02_forward_in0"):
+        gather.forward(0, 0)
+    with scope("p03_norm0"):
+        filter_map(0, 20, 32)
+        normalise(0)
+    with scope("p04_finish_in0"):
+        gather.finish(0, 0)
+    with scope("p05_expand0"):
+        expand(0, False, 0, 5)
+    with scope("p05_forward_out0"):
+        gather.forward(0, 1)
+    with scope("p05_expand0b"):
+        expand(0, False, 5)
+    with scope("p06_finish_out0"):
+        gather.finish(0, 1)
+    with scope("p06_contract0"):
+        contract(0)
+        residual(0, middle)
+        fill(padded1, middle)
+    with scope("p07_halo1"):
+        halos[1].start()
+        gather.start(1, 1)
+        gather.forward(1, 0)
+    with scope("p08_halo1_end"):
+        halos[1].finish()
+    with scope("p09_depth1"):
+        filter_map(1, 0, 32)
+        normalise(1)
+    with scope("p10_weights1"):
+        gather.finish(1, 0)
+        gather.forward(1, 1)
+        gather.finish(1, 1)
+    with scope("p11_expand1"):
+        expand(1, True)
+    with scope("p12_ngrads1"):
+        normal_grads(1, upstream)
+    with scope("p13_leave1"):
+        leave(1, upstream)
+        halos[2].start()
+    out1, in1 = reducing(1)
+    out0, in0 = reducing(0)
+    little = ways[Small, None]
+
+    def go(name, *group):
+        with scope(name):
+            for way in group:
+                way.advance()
+
+    with scope("p14_wgrads1"):
+        weight_grads(1)
+    go("p14_go1", out1, in1)
+    with scope("p16_halo2_end"):
+        halos[2].finish()
+    with scope("p17_depth1"):
+        depthwise(padded_g1, taps.at[1], result, True, 0, 10)
+    go("p17_go1", out1, in1)
+    with scope("p17_depth1b"):
+        depthwise(padded_g1, taps.at[1], result, True, 10, 32)
+        for r in range(16):
+            rows = slice(r * 32, r * 32 + 32)
+            upstream[rows, :] = from_cotangent(rows) + pixels(result, r)
+    with scope("p18_enter0"):
+        enter(0, from_upstream)
+        scale_grad(0, from_upstream)
 
     def chunk(c, _):
         cols = part(c * CHUNK, CHUNK)
@@ -746,58 +826,62 @@
         keep_hidden_grad(0, c, cols, grads)
         return 0
 
-    lax.fori_loop(0, 2048 // CHUNK, chunk, 0)
-    for way in reducing(1):
-        way.split_finish(1)
-        way.across_start()
-    weight_grads(0)
-    for way in reducing(0):
-        way.core_start()
-    normal_grads(0, branch.at[1])
-    for way in reducing(1):
-        way.across_finish()
-        way.join_start(1)
-    for way in reducing(0):
-        way.core_finish()
-        way.split_start(0)
-    leave(0, branch.at[1])
-    halos[3].start()
-    settle(0)
-    for way in reducing(1):
-        way.join_finish(1)
-        way.join_start(0)
-    tap_grads(padded0, padded_g, small, 0)
-    ways[Small, None].core_start()
-    halos[3].finish()
-    depthwise(padded_g, taps.at[0], result, True)
-    for r in range(16):
-        rows = slice(r * 32, r * 32 + 32)
-        grad_slides[rows, :] = (upstream[rows, :] + pixels(result, r)).astype(BF)
-    for way in reducing(1):
-        way.join_finish(0)
-        way.share_start()
-    last = [ways[Small, None]] + reducing(0)
-    last[0].core_finish()
-    last[0].split_start(0)
-    for way in last:
-        way.split_finish(0)
-        way.split_start(1)
-    for way in last:
-        way.split_finish(1)
-        way.across_start()
-    for way in last:
-        way.across_finish()
-        way.join_start(1)
-    for way in last:
-        way.join_finish(1)
-        way.join_start(0)
-    for way in last:
-        way.join_finish(0)
-        way.share_start()
-    for way in reducing(1) + last:
-        way.share_finish()
-    for way in reducing(1) + last + halos + [gather]:
-        way.drain()
+    with scope("p19_hidden0"):
+        lax.fori_loop(0, 2048 // CHUNK, chunk, 0)
+    go("p20_go1", out1)
+    with scope("p21_wgrads0"):
+        weight_grads(0)
+    go("p21_go0", out0, in0)
+    go("p22_go1", in1, out1)
+    with scope("p23_ngrads0"):
+        normal_grads(0, normed.at[1])
+    with scope("p24_leave0"):
+        leave(0, normed.at[1])
+        halos[3].start()
+    go("p25_go0", out0, in0)
+    with scope("p26_contract1"):
+        contract(1)
+        residual(1, output)
+        scale_grad(1, from_cotangent)
+        settle(1)
+        settle(0)
+    go("p27_go1", in1, out1)
+    with scope("p28_taps0"):
+        tap_grads(padded0, padded_g0, small, 0, range(7))
+    go("p29_go0", out0)
+    with scope("p29_taps1"):
+        tap_grads(padded1, padded_g1, small, 64, range(3))
+    go("p29_go0b", in0, in1, out1)
+    with scope("p29_taps1b"):
+        tap_grads(padded1, padded_g1, small, 64, range(3, 7))
+    little.advance()
+    go("p30_go0", out0)
+    with scope("p30_halo3_end"):
+        halos[3].finish()
+    with scope("p31_depth0"):
+        depthwise(padded_g0, taps.at[0], result, True, 0, 12)
+    go("p31_go", little, in0, out0)
+    with scope("p33_depth0"):
+        depthwise(padded_g0, taps.at[0], result, True, 12, 24)
+    go("p33_go", little, in0)
+    with scope("p33_depth0b"):
+        depthwise(padded_g0, taps.at[0], result, True, 24, 32)
+        for r in range(16):
+            rows = slice(r * 32, r * 32 + 32)
+            grad_slides[rows, :] = (upstream[rows, :] + pixels(result, r)).astype(BF)
+    go("p34_go", little, in0, out0, in1, out1)
+    go("p35_go", little, in0, out0, in1, out1)
+    go("p36_go", little, in0, out0, in1, out1)
+    go("p37_go", little, in0)
+    every = [out1, in1, little, out0, in0]
+    with scope("p38_rest"):
+        while any(way.steps for way in every):
+            for way in every:
+                if way.steps:
+                    way.advance()
+    with scope("p39_drain"):
+        for way in every + halos + [gather]:
+            way.drain()
 
 
 def halo_scratch():
@@ -811,12 +895,13 @@
     ]
 
 
-def whole_step(slides, cotangent, kernel, channel, bias_in, weight_in, weight_out):
+def whole_step(*operands):
     vmem = pl.BlockSpec(memory_space=pltpu.VMEM)
     grid = pltpu.VMEM((BACK * SPAN * 8, 128), F32)
     scratch = [
         pltpu.VMEM((2, 512, 2048), BF),
         pltpu.VMEM((2, 2048, 512), BF),
+        grid,
         grid,
         grid,
         grid,
@@ -830,7 +915,7 @@
         pltpu.VMEM((512, 2048), BF),
         pltpu.VMEM((512, 2048), BF),
         pltpu.VMEM((2, 512, 512), F32),
-        pltpu.VMEM((5, 8, 512), F32),
+        pltpu.VMEM((2, 5, 8, 512), F32),
         pltpu.VMEM((512, 512), F32),
         pltpu.VMEM((512, 512), BF),
         pltpu.VMEM((2, 512, 512), BF),
@@ -844,7 +929,7 @@
     for _ in range(4):
         scratch += halo_scratch()
     extra = [pltpu.VMEM((2, 2048), F32)]
-    reductions = sum([reduction_scratch(kind) for kind, _ in UNITS], [])
+    reductions = sum([reduction_scratch(kind, early) for kind, _, early in UNITS], [])
     return pl.pallas_call(
         step_kernel,
         out_shape=(
@@ -854,14 +939,79 @@
             jax.ShapeDtypeStruct((2, 2048, 256), BF),
             jax.ShapeDtypeStruct((128, 512), F32),
         ),
-        in_specs=[vmem] * 5 + [pl.BlockSpec(memory_space=pl.ANY)] * 2,
+        in_specs=[vmem] * 9 + [pl.BlockSpec(memory_space=pl.ANY)] * 2,
         out_specs=[vmem] * 5,
         scratch_shapes=scratch + extra + reductions,
         compiler_params=pltpu.CompilerParams(
             collective_id=0, has_side_effects=True, vmem_limit_bytes=67043328
         ),
         name="whole_step",
-    )(slides, cotangent, kernel, channel, bias_in, weight_in, weight_out)
+    )(*operands)
+
+
+def unpack_kernel(
+    output, grad_slides, total_in, total_out, small,
+    output_end, slides_end, in_end, out_end, kernel_end, channel_end, bias_end,
+    maps, low_in, low_out, wide_in, wide_out, get, put,
+):
+    steps = []
+    for which in range(2):
+        for cut in range(4):
+            for ends, size in (
+                ((total_in, low_in, wide_in, in_end), 64),
+                ((total_out, low_out, wide_out, out_end), 512),
+            ):
+                steps.append([ref.at[which, pl.ds(cut * size, size), :] for ref in ends])
+    steps.append([output, maps.at[0], maps.at[0], output_end])
+    steps.append([grad_slides, maps.at[1], maps.at[1], slides_end])
+    for number, (src, low, _, _) in enumerate(steps):
+        pltpu.make_async_copy(src, low, get.at[number]).start()
+    for number, (src, low, wide, dst) in enumerate(steps):
+        pltpu.make_async_copy(src, low, get.at[number]).wait()
+        if number < 16:
+            wide[...] = low[...].astype(F32)
+        pltpu.make_async_copy(wide, dst, put.at[number]).start()
+    for which in range(2):
+        base = which * 64
+        for p in range(7):
+            kernel_end[p, :, which, :] = small[base + p * 7 : base + p * 7 + 7, :]
+        channel_end[:, which, :] = small[base + 49 : base + 54, :]
+        for c in range(4):
+            bias_end[which : which + 1, c * 512 : c * 512 + 512] = small[
+                base + 54 + c : base + 55 + c, :
+            ]
+    for number, (_, _, wide, dst) in enumerate(steps):
+        pltpu.make_async_copy(wide, dst, put.at[number]).wait()
+
+
+def unpack(*results):
+    vmem = pl.BlockSpec(memory_space=pltpu.VMEM)
+    hbm = pl.BlockSpec(memory_space=pl.ANY)
+    return pl.pallas_call(
+        unpack_kernel,
+        out_shape=(
+            jax.ShapeDtypeStruct((512, 512), BF),
+            jax.ShapeDtypeStruct((512, 512), BF),
+            jax.ShapeDtypeStruct((2, 256, 2048), F32),
+            jax.ShapeDtypeStruct((2, 2048, 256), F32),
+            jax.ShapeDtypeStruct((7, 7, 2, 512), F32),
+            jax.ShapeDtypeStruct((5, 2, 512), F32),
+            jax.ShapeDtypeStruct((2, 2048), F32),
+        ),
+        in_specs=[hbm] * 4 + [vmem],
+        out_specs=[hbm] * 4 + [vmem] * 3,
+        scratch_shapes=[
+            pltpu.VMEM((2, 512, 512), BF),
+            pltpu.VMEM((2, 256, 2048), BF),
+            pltpu.VMEM((2, 2048, 256), BF),
+            pltpu.VMEM((2, 256, 2048), F32),
+            pltpu.VMEM((2, 2048, 256), F32),
+            pltpu.SemaphoreType.DMA((18,)),
+            pltpu.SemaphoreType.DMA((18,)),
+        ],
+        compiler_params=pltpu.CompilerParams(vmem_limit_bytes=67043328),
+        name="unpack",
+    )(*results)
 
 
 def per_device(
@@ -878,25 +1028,28 @@
     layer_scale,
 ):
     channels = slides.shape[-1]
-    channel = jnp.stack([kernel_bias, norm_gain, norm_bias, bias_out, layer_scale], axis=1)
-    output, grad_slides, total_in, total_out, small = whole_step(
+    results = whole_step(
         slides.reshape(-1, channels),
         cotangent.reshape(-1, channels),
-        kernel.reshape(2, 49, channels),
-        channel,
+        kernel.transpose(1, 2, 0, 3),
+        kernel_bias,
+        norm_gain,
+        norm_bias,
+        bias_out,
+        layer_scale,
         bias_in,
         weight_in,
         weight_out,
     )
-    small = small.reshape(2, 64, channels)
+    output, grad_slides, total_in, total_out, taps, sums, biases = unpack(*results)
     return (
         output.reshape(slides.shape),
         grad_slides.reshape(slides.shape),
-        total_in.astype(F32),
-        total_out.astype(F32),
-        small[:, :49].reshape(2, 7, 7, channels),
-        small[:, 49:54],
-        small[:, 54:58].reshape(2, 4 * channels),
+        total_in,
+        total_out,
+        taps.transpose(2, 0, 1, 3),
+        sums.transpose(1, 0, 2),
+        biases,
     )
 
 

time: 164 us -> 136 us (0.83)
  local copies, waits for them, and re-layouts: 12 us -> 0 us
  Pallas kernels: 144 us -> 135 us
  other arithmetic: 6.62 us -> 0 us
    pallas_call x1, Pallas kernels: 144 us -> 128 us  [whole_step(): pl.pallas_call(step_kernel, out_shape=(jax.ShapeDtypeStruct((512, 512), B...]
    pallas_call x0 -> x1, Pallas kernels: none -> 6.63 us  [unpack(): pl.pallas_call(unpack_kernel, out_shape=(jax.ShapeDtypeStruct((512, 512),...]
    convert_element_type x2 -> x0, other arithmetic: 6.62 us -> none  [the longest x1 4.28 us: per_device(): total_in.astype(F32)]
    another operation x6 -> x0, local copies, waits for them, and re-layouts: 4.1 us -> none  [per_device(): jnp.stack([kernel_bias, norm_gain, norm_bias, bias_out, layer_scale], axi...]
    unnamed x11 -> x0, local copies, waits for them, and re-layouts: 3.69 us -> none
    slice x3 -> x0, local copies, waits for them, and re-layouts: 2.55 us -> none  [the longest x2 1.79 us: per_device(): small[:, :49].reshape(2, 7, 7, channels)]
    reshape x1 -> x0, local copies, waits for them, and re-layouts: 1.66 us -> none  [per_device(): kernel.reshape(2, 49, channels)]
where the time goes in v2:
time: 136 us
  Pallas kernels  135 us (99%)
    pallas_call x1, Pallas kernels, whole_step(): pl.pallas_call(step_kernel, out_shape=(jax.ShapeDtypeStruct((512, 512), B...  128 us
    pallas_call x1, Pallas kernels, unpack(): pl.pallas_call(unpack_kernel, out_shape=(jax.ShapeDtypeStruct((512, 512),...  6.63 us

profile of v2, /device:TPU:1, one launch (start us, length us, event | category | flops | bytes accessed | tf_op | source)
XLA Modules:
  0.0 135.7 jit_solution(13303774886453752157)
XLA Ops:
  0.6 128.2 %whole_step.1 = (bf16[512,512]{1,0:T(8,128)(2,1)}, bf16[512,512]{1,0:T(8,128)(2,1)}, bf16[2,256,2048]{2,1,0:T(8,128)(2,1)}, bf16[2,2048,256]{2,1,0:T(8,128)(2,1)}, f32[128,512]{1,0:T(8,128)}) custom-call(bf16[512,512]{1,0:T(8,128)(2,1)} %bitcast.7, bf16[512,512]{1,0:T(8,128)(2,1)} %bitcast.8, f32[7,7,2,512]{3,2,1,0:T(2,128)} %bitcast.9, ...), custom_call_target="tpu_custom_call" | custom-call | tf_op jit(solution)/shard_map/whole_step/pallas_call | solution.py:933
  128.9 6.6 %unpack.1 = (bf16[512,512]{1,0:T(8,128)(2,1)}, bf16[512,512]{1,0:T(8,128)(2,1)}, f32[2,256,2048]{2,1,0:T(8,128)}, f32[2,2048,256]{2,1,0:T(8,128)}, f32[7,7,2,512...) custom-call(bf16[512,512]{1,0:T(8,128)(2,1)} %get-tuple-element.19.output, ...), custom_call_target="tpu_custom_call" | custom-call | tf_op jit(solution)/shard_map/unpack/pallas_call | solution.py:990

commit v3 on v2

--- a/solution.py
+++ b/solution.py
@@ -114,38 +114,11 @@
         return final.at[:, part(core * 128, 128)]
 
 
-class Small:
-    received = (64, 512)
-    turn = (32, 512)
-    first = (32, 128)
-    second = (8, 128)
-    third = (8, 128)
-
-    def offered(grad, half, core):
-        return grad.at[part(core * 64, 64), :]
-
-    def cut(got, halves, turn, index):
-        return got.at[halves, turn * 32 : turn * 32 + 32, part(index * 128, 128)]
-
-    def cut_again(block, index):
-        return block.at[:, part(index * 8, 8), :]
-
-    def placed(final, core, turn, one, two):
-        return final.at[part(core * 64 + turn * 32 + two * 8, 8), part(one * 128, 128)]
-
-    def line(final, core, turn, one):
-        return final.at[part(core * 64 + turn * 32, 32), part(one * 128, 128)]
-
-    def of_core(final, core):
-        return final.at[part(core * 64, 64), :]
-
-
 class Reduction:
     def __init__(self, me, kind, early, grad, final, bufs, sems):
         self.me, self.kind, self.early, self.grad, self.final = me, kind, early, grad, final
         self.got, self.given, self.r1, self.b1, self.r2, self.b2, self.r3 = bufs
         self.sems = sems
-        self.halves = 1 if kind is Small else 2
         self.copies = []
         self.steps = [
             [self.core_start],
@@ -183,12 +156,12 @@
         ).wait_recv()
 
     def core_start(self):
-        for half in range(self.halves):
+        for half in range(2):
             src = self.kind.offered(self.grad, half, 1 - self.me.core)
             self.go(src, self.got.at[half], 0, 0, half, half, self.me.sibling())
 
     def core_finish(self):
-        for half in range(self.halves):
+        for half in range(2):
             self.landed(self.got.at[half], 0, 0, half)
             own = self.kind.offered(self.grad, half, self.me.core)
             total = own[...].astype(F32) + self.got[half].astype(F32)
@@ -251,9 +224,9 @@
                 continue
             for offset in (1, 3, 2):
                 index, device = self.me.along("x", offset)
-                src = block.at[lax.rem(index, 2) if self.halves == 2 else 0]
+                src = block.at[lax.rem(index, 2)]
                 self.go(src, self.r3.at[turn, self.me.x], turn, 3, offset, self.me.x, device)
-            self.r3[turn, self.me.x] = block[self.me.half if self.halves == 2 else 0]
+            self.r3[turn, self.me.x] = block[self.me.half]
 
     def across_finish(self):
         me = self.me
@@ -309,24 +282,119 @@
             copy.wait_send()
 
 
+class SmallReduction:
+    def __init__(self, me, grad, final, bufs, sems):
+        self.me, self.grad, self.final = me, grad, final
+        self.got, self.parts, self.lines = bufs
+        self.sems = sems
+        self.copies = []
+        self.steps = [
+            self.core_start,
+            self.plane_start,
+            self.across_start,
+            self.join_start,
+            self.share_start,
+            self.share_finish,
+        ]
+
+    def advance(self):
+        self.steps.pop(0)()
+
+    def drain(self):
+        for copy in self.copies:
+            copy.wait_send()
+
+    def go(self, src, dst, slot, target):
+        copy = remote(src, dst, self.sems.at[0, slot], self.sems.at[1, slot], target)
+        copy.start()
+        self.copies.append(copy)
+
+    def landed(self, dst, slot):
+        target = self.me.sibling()
+        remote(dst, dst, self.sems.at[0, slot], self.sems.at[1, slot], target).wait_recv()
+
+    def others(self):
+        for up in range(4):
+            for deep in range(4):
+                if up or deep:
+                    y = lax.rem(self.me.y + up, 4)
+                    z = lax.rem(self.me.z + deep, 4)
+                    yield up * 4 + deep, y, z, self.me.device(y=y, z=z)
+
+    def cell(self, ref, row, y, z):
+        return ref.at[part(row + y * 16, 16), part(z * 128, 128)]
+
+    def core_start(self):
+        src = self.grad.at[part((1 - self.me.core) * 64, 64), :]
+        self.go(src, self.got, 0, self.me.sibling())
+
+    def plane_start(self):
+        self.landed(self.got, 0)
+        own = self.grad[part(self.me.core * 64, 64), :]
+        self.got[...] = own + self.got[...]
+        for slot, y, z, device in self.others():
+            self.go(self.cell(self.got, 0, y, z), self.parts.at[slot], slot, device)
+
+    def across_start(self):
+        me = self.me
+        total = self.cell(self.got, 0, me.y, me.z)[...]
+        for slot, _, _, _ in self.others():
+            self.landed(self.parts.at[slot], slot)
+            total = total + self.parts[slot]
+        self.lines[me.x] = total
+        for offset in (1, 3, 2):
+            _, device = me.along("x", offset)
+            copy = remote(
+                self.lines.at[me.x],
+                self.lines.at[me.x],
+                self.sems.at[0, 15 + offset],
+                self.sems.at[1, 32 + me.x],
+                device,
+            )
+            copy.start()
+            self.copies.append(copy)
+
+    def join_start(self):
+        me = self.me
+        for offset in (1, 3, 2):
+            index, _ = me.along("x", offset)
+            self.landed(self.lines.at[index], 32 + index)
+        total = self.lines[0] + self.lines[1] + (self.lines[2] + self.lines[3])
+        block = self.cell(self.final, me.core * 64, me.y, me.z)
+        block[...] = total
+        for slot, _, _, device in self.others():
+            self.go(block, block, 40 + slot, device)
+
+    def share_start(self):
+        me = self.me
+        for slot, _, _, _ in self.others():
+            y = lax.rem(me.y + 4 - slot // 4, 4)
+            z = lax.rem(me.z + 4 - slot % 4, 4)
+            self.landed(self.cell(self.final, me.core * 64, y, z), 40 + slot)
+        block = self.final.at[part(me.core * 64, 64), :]
+        self.go(block, block, 60, me.sibling())
+
+    def share_finish(self):
+        block = self.final.at[part((1 - self.me.core) * 64, 64), :]
+        self.landed(block, 60)
+
+
 def reduction_scratch(kind, early):
-    dtype = F32 if kind is Small else BF
-    halves = 1 if kind is Small or early else 2
+    halves = 1 if early else 2
     return [
-        pltpu.VMEM((1 if kind is Small else 2, *kind.received), dtype),
-        pltpu.VMEM((2, *kind.turn) if early else (2, 8, 128), dtype),
-        pltpu.VMEM((2, 3, halves, *kind.first), dtype),
-        pltpu.VMEM((2, halves, *kind.first), dtype),
-        pltpu.VMEM((2, 3, halves, *kind.second), dtype),
-        pltpu.VMEM((2, halves, *kind.second), dtype),
-        pltpu.VMEM((2, 4, *kind.third), dtype),
+        pltpu.VMEM((2, *kind.received), BF),
+        pltpu.VMEM((2, *kind.turn) if early else (2, 8, 128), BF),
+        pltpu.VMEM((2, 3, halves, *kind.first), BF),
+        pltpu.VMEM((2, halves, *kind.first), BF),
+        pltpu.VMEM((2, 3, halves, *kind.second), BF),
+        pltpu.VMEM((2, halves, *kind.second), BF),
+        pltpu.VMEM((2, 4, *kind.third), BF),
         pltpu.SemaphoreType.DMA((2, 64)),
     ]
 
 
 UNITS = (
-    (Small, None, False),
-    (WeightOut, 1, True),
+    (WeightOut, 1, False),
     (WeightIn, 1, True),
     (WeightOut, 0, False),
     (WeightIn, 0, True),
@@ -504,21 +572,76 @@
 
 
 def depthwise(padded, taps, result, flipped, first=0, last=32):
+    def columns(pair, _):
+        j = pair * 2
+        totals = [[None] * FRONT for _ in range(2)]
+        for c in range(8):
+            values = [padded[word(i, j + c), :] for i in range(BACK)]
+            for side in range(2):
+                q = c - side
+                if not 0 <= q < 7:
+                    continue
+                total = totals[side]
+                for p in range(7):
+                    number = (6 - p) * 7 + 6 - q if flipped else p * 7 + q
+                    tap = taps[number * 8 : number * 8 + 8, :]
+                    for i in range(FRONT):
+                        term = values[i + p] * tap
+                        total[i] = term if total[i] is None else total[i] + term
+        for side in range(2):
+            for i in range(FRONT):
+                result[pl.ds(pl.multiple_of((i * 32 + j + side) * 8, 8), 8), :] = totals[side][i]
+        return 0
+
+    lax.fori_loop(first // 2, last // 2, columns, 0)
+
+
+def add_rim(padded, taps, result):
+    place = lax.broadcasted_iota(jnp.int32, (8, 128), 0)
+    top = jnp.where(place < 4, 1.0, 0.0).astype(F32)
+    bottom = 1.0 - top
+
+    def tap_of(p, q):
+        return taps[(p * 7 + q) * 8 : (p * 7 + q) * 8 + 8, :]
+
+    def add(i, j, value):
+        start = (i * 32 + j) * 8
+        at = pl.ds(start if isinstance(start, int) else pl.multiple_of(start, 8), 8)
+        result[at, :] = result[at, :] + value
+
+    def rows_of(j, columns):
+        for base, mask, outs in ((0, top, (0, 1, 2)), (11, bottom, (5, 6, 7))):
+            totals = {}
+            for q in columns:
+                for line in range(3):
+                    value = padded[word(base + line, j + q), :] * mask
+                    for i in outs:
+                        p = base + line - i
+                        if 0 <= p < 7:
+                            term = value * tap_of(p, q)
+                            totals[i] = term if i not in totals else totals[i] + term
+            for i in outs:
+                add(i, j, totals[i])
+
     def column(j, _):
-        total = [None] * FRONT
+        rows_of(j, range(7))
+        return 0
+
+    lax.fori_loop(3, 29, column, 0)
+    for j in (0, 1, 2, 29, 30, 31):
+        inner = [q for q in range(7) if 3 <= j + q < 35]
+        rows_of(j, inner)
+        totals = [None] * FRONT
         for q in range(7):
+            if q in inner:
+                continue
             values = [padded[word(i, j + q), :] for i in range(BACK)]
             for p in range(7):
-                number = (6 - p) * 7 + 6 - q if flipped else p * 7 + q
-                tap = taps[number * 8 : number * 8 + 8, :]
                 for i in range(FRONT):
-                    term = values[i + p] * tap
-                    total[i] = term if total[i] is None else total[i] + term
+                    term = values[i + p] * tap_of(p, q)
+                    totals[i] = term if totals[i] is None else totals[i] + term
         for i in range(FRONT):
-            result[pl.ds(pl.multiple_of((i * 32 + j) * 8, 8), 8), :] = total[i]
-        return 0
-
-    lax.fori_loop(first, last, column, 0)
+            add(i, j, totals[i])
 
 
 def tap_grads(padded, upstream, small, base, columns):
@@ -536,7 +659,7 @@
             return tuple(result)
 
         zero = jnp.zeros((8, 128), F32)
-        totals = lax.fori_loop(0, 32, column, (zero,) * 7)
+        totals = lax.fori_loop(0, 32, column, (zero,) * 7, unroll=4)
         for p in range(7):
             both = totals[p][:4] + totals[p][4:]
             for group in range(4):
@@ -594,14 +717,14 @@
     for number, (kind, which, early) in enumerate(UNITS):
         bufs = scratch[number * 8 : number * 8 + 7]
         sems = scratch[number * 8 + 7]
-        if kind is Small:
-            ends = (small, final_small)
-        elif kind is WeightIn:
+        if kind is WeightIn:
             ends = (grad_in.at[which], final_in.at[which])
         else:
             ends = (grad_out.at[which], final_out.at[which])
         ways[kind, which] = Reduction(me, kind, early, *ends, bufs, sems)
 
+    little = SmallReduction(me, small, final_small, scratch[-4:-1], scratch[-1])
+
     def reducing(which):
         return [ways[WeightOut, which], ways[WeightIn, which]]
 
@@ -618,11 +741,14 @@
         for r in range(16):
             put_row(grid, r + 3, 3, tile[r * 32 : r * 32 + 32, :].astype(F32))
 
-    partners = [me.along(axis, offset)[1] for axis in "xyz" for offset in (1, 2, 3)]
+    partners = [me.along("x", offset)[1] for offset in (1, 2, 3)]
+    partners += [device for _, _, _, device in little.others()]
     around = [
         halos[0].target(down, right) for down in (-1, 0, 1) for right in (-1, 0, 1) if down
     ]
     with scope("p00a_fill"):
+        padded0[...] = jnp.zeros_like(padded0)
+        padded1[...] = jnp.zeros_like(padded1)
         fill(padded0, slides)
         for which in range(2):
             spread_taps(kernel, which, taps.at[which])
@@ -650,20 +776,29 @@
             rstd[which, rows, :] = jnp.broadcast_to(inverse, (32, 128))
             normal[which, rows, :] = (values * line(which, norm_gain) + line(which, norm_bias)).astype(BF)
 
-    def expand(which, with_grad, first=0, last=2048 // CHUNK):
+    def expand(which, tilts, first=0, last=2048 // CHUNK):
         def chunk(c, _):
             cols = part(c * CHUNK, CHUNK)
             hidden = dot(normal[which], full_in[which, :, cols]) + bias_in[which : which + 1, cols]
             value, tilt = gelu_and_slope(hidden)
             act[which, :, cols] = value.astype(BF)
-            if with_grad:
+            if tilts is None:
                 grads = dot(low[...], full_out[which, cols, :], 1, 1) * tilt
                 keep_hidden_grad(which, c, cols, grads)
             else:
-                slope[:, cols] = tilt.astype(BF)
+                tilts[:, cols] = tilt.astype(BF)
             return 0
 
         lax.fori_loop(first, last, chunk, 0)
+
+    def hidden_grads(which, tilts, last):
+        def chunk(c, _):
+            cols = part(c * CHUNK, CHUNK)
+            grads = dot(low[...], full_out[which, cols, :], 1, 1) * tilts[:, cols].astype(F32)
+            keep_hidden_grad(which, c, cols, grads)
+            return 0
+
+        lax.fori_loop(0, last, chunk, 0)
 
     def keep_hidden_grad(which, c, cols, grads):
         hidden_grad[:, cols] = grads.astype(BF)
@@ -750,24 +885,25 @@
     def from_upstream(rows):
         return upstream[rows, :]
 
-    with scope("p00e_halo0"):
+    with scope("p01_depth0"):
         enter(1, from_cotangent)
+        filter_map(0, 0, 32)
+    with scope("p01_halo0"):
         halos[0].finish()
-    with scope("p01_depth0"):
-        filter_map(0, 0, 20)
+    with scope("p01_rim0"):
+        add_rim(padded0, taps.at[0], result)
     with scope("p02_forward_in0"):
         gather.forward(0, 0)
     with scope("p03_norm0"):
-        filter_map(0, 20, 32)
         normalise(0)
     with scope("p04_finish_in0"):
         gather.finish(0, 0)
     with scope("p05_expand0"):
-        expand(0, False, 0, 5)
+        expand(0, slope, 0, 5)
     with scope("p05_forward_out0"):
         gather.forward(0, 1)
     with scope("p05_expand0b"):
-        expand(0, False, 5)
+        expand(0, slope, 5)
     with scope("p06_finish_out0"):
         gather.finish(0, 1)
     with scope("p06_contract0"):
@@ -778,17 +914,26 @@
         halos[1].start()
         gather.start(1, 1)
         gather.forward(1, 0)
+    with scope("p08_depth1"):
+        filter_map(1, 0, 32)
     with scope("p08_halo1_end"):
         halos[1].finish()
-    with scope("p09_depth1"):
-        filter_map(1, 0, 32)
+    with scope("p09_norm1"):
+        add_rim(padded1, taps.at[1], result)
         normalise(1)
-    with scope("p10_weights1"):
+    with scope("p09_finish_in1"):
         gather.finish(1, 0)
+    with scope("p10_expand1"):
+        expand(1, hidden_grad, 0, 2)
+    with scope("p10_forward_out1"):
         gather.forward(1, 1)
+    with scope("p10_expand1b"):
+        expand(1, hidden_grad, 2, 4)
+    with scope("p10_finish_out1"):
         gather.finish(1, 1)
     with scope("p11_expand1"):
-        expand(1, True)
+        expand(1, None, 4)
+        hidden_grads(1, hidden_grad, 4)
     with scope("p12_ngrads1"):
         normal_grads(1, upstream)
     with scope("p13_leave1"):
@@ -796,7 +941,6 @@
         halos[2].start()
     out1, in1 = reducing(1)
     out0, in0 = reducing(0)
-    little = ways[Small, None]
 
     def go(name, *group):
         with scope(name):
@@ -805,7 +949,8 @@
 
     with scope("p14_wgrads1"):
         weight_grads(1)
-    go("p14_go1", out1, in1)
+        out1.advance()
+        in1.advance()
     with scope("p16_halo2_end"):
         halos[2].finish()
     with scope("p17_depth1"):
@@ -820,25 +965,21 @@
         enter(0, from_upstream)
         scale_grad(0, from_upstream)
 
-    def chunk(c, _):
-        cols = part(c * CHUNK, CHUNK)
-        grads = dot(low[...], full_out[0, cols, :], 1, 1) * slope[:, cols].astype(F32)
-        keep_hidden_grad(0, c, cols, grads)
-        return 0
-
     with scope("p19_hidden0"):
-        lax.fori_loop(0, 2048 // CHUNK, chunk, 0)
-    go("p20_go1", out1)
+        hidden_grads(0, slope, 2048 // CHUNK)
+    go("p20_go1", out1, in1)
     with scope("p21_wgrads0"):
         weight_grads(0)
-    go("p21_go0", out0, in0)
-    go("p22_go1", in1, out1)
+    in0.advance()
+    out0.advance()
     with scope("p23_ngrads0"):
         normal_grads(0, normed.at[1])
+    go("p23_go1", out1, in1)
+    go("p23_go0", in0)
     with scope("p24_leave0"):
         leave(0, normed.at[1])
         halos[3].start()
-    go("p25_go0", out0, in0)
+    go("p25_go0", out0)
     with scope("p26_contract1"):
         contract(1)
         residual(1, output)
@@ -848,31 +989,29 @@
     go("p27_go1", in1, out1)
     with scope("p28_taps0"):
         tap_grads(padded0, padded_g0, small, 0, range(7))
-    go("p29_go0", out0)
+    go("p29_go0", in0)
+    go("p29_go1", in1)
     with scope("p29_taps1"):
-        tap_grads(padded1, padded_g1, small, 64, range(3))
-    go("p29_go0b", in0, in1, out1)
-    with scope("p29_taps1b"):
-        tap_grads(padded1, padded_g1, small, 64, range(3, 7))
+        tap_grads(padded1, padded_g1, small, 64, range(7))
     little.advance()
-    go("p30_go0", out0)
+    go("p30_go0", in0)
+    go("p30_go0b", out0)
+    go("p30_go1", out1, in1)
     with scope("p30_halo3_end"):
         halos[3].finish()
     with scope("p31_depth0"):
-        depthwise(padded_g0, taps.at[0], result, True, 0, 12)
+        depthwise(padded_g0, taps.at[0], result, True, 0, 16)
     go("p31_go", little, in0, out0)
     with scope("p33_depth0"):
-        depthwise(padded_g0, taps.at[0], result, True, 12, 24)
-    go("p33_go", little, in0)
+        depthwise(padded_g0, taps.at[0], result, True, 16, 32)
+    go("p33_go", in0, little, out0)
     with scope("p33_depth0b"):
-        depthwise(padded_g0, taps.at[0], result, True, 24, 32)
         for r in range(16):
             rows = slice(r * 32, r * 32 + 32)
             grad_slides[rows, :] = (upstream[rows, :] + pixels(result, r)).astype(BF)
-    go("p34_go", little, in0, out0, in1, out1)
-    go("p35_go", little, in0, out0, in1, out1)
-    go("p36_go", little, in0, out0, in1, out1)
-    go("p37_go", little, in0)
+    go("p34_go", in0, little, out0, out1, in1)
+    go("p35_go", in0, little, out0)
+    go("p36_go", in0, little, out0, out1, in1)
     every = [out1, in1, little, out0, in0]
     with scope("p38_rest"):
         while any(way.steps for way in every):
@@ -930,6 +1069,12 @@
         scratch += halo_scratch()
     extra = [pltpu.VMEM((2, 2048), F32)]
     reductions = sum([reduction_scratch(kind, early) for kind, _, early in UNITS], [])
+    reductions += [
+        pltpu.VMEM((64, 512), F32),
+        pltpu.VMEM((16, 16, 128), F32),
+        pltpu.VMEM((4, 16, 128), F32),
+        pltpu.SemaphoreType.DMA((2, 64)),
+    ]
     return pl.pallas_call(
         step_kernel,
         out_shape=(

time: 136 us -> 129 us (0.949)
  Pallas kernels: 135 us -> 128 us
    pallas_call x1, Pallas kernels: 128 us -> 122 us  [whole_step(): pl.pallas_call(step_kernel, out_shape=(jax.ShapeDtypeStruct((512, 512), B...]
where the time goes in v3:
time: 129 us
  Pallas kernels  128 us (99%)
    pallas_call x1, Pallas kernels, whole_step(): pl.pallas_call(step_kernel, out_shape=(jax.ShapeDtypeStruct((512, 512), B...  122 us
    pallas_call x1, Pallas kernels, unpack(): pl.pallas_call(unpack_kernel, out_shape=(jax.ShapeDtypeStruct((512, 512),...  6.63 us

profile of v3, /device:TPU:1, one launch (start us, length us, event | category | flops | bytes accessed | tf_op | source)
XLA Modules:
  0.0 129.1 jit_solution(15798482613286345046)
XLA Ops:
  0.6 121.6 %whole_step.1 = (bf16[512,512]{1,0:T(8,128)(2,1)}, bf16[512,512]{1,0:T(8,128)(2,1)}, bf16[2,256,2048]{2,1,0:T(8,128)(2,1)}, bf16[2,2048,256]{2,1,0:T(8,128)(2,1)}, f32[128,512]{1,0:T(8,128)}) custom-call(bf16[512,512]{1,0:T(8,128)(2,1)} %bitcast.7, bf16[512,512]{1,0:T(8,128)(2,1)} %bitcast.8, f32[7,7,2,512]{3,2,1,0:T(2,128)} %bitcast.9, ...), custom_call_target="tpu_custom_call" | custom-call | tf_op jit(solution)/shard_map/whole_step/pallas_call | solution.py:1078
  122.3 6.6 %unpack.1 = (bf16[512,512]{1,0:T(8,128)(2,1)}, bf16[512,512]{1,0:T(8,128)(2,1)}, f32[2,256,2048]{2,1,0:T(8,128)}, f32[2,2048,256]{2,1,0:T(8,128)}, f32[7,7,2,512...) custom-call(bf16[512,512]{1,0:T(8,128)(2,1)} %get-tuple-element.19.output, ...), custom_call_target="tpu_custom_call" | custom-call | tf_op jit(solution)/shard_map/unpack/pallas_call | solution.py:1135

commit v4 on v3

--- a/solution.py
+++ b/solution.py
@@ -683,10 +683,10 @@
 
 def gelu_and_slope(values):
     square = values * values
-    tangent = jnp.tanh(COEF * values * (1.0 + CUBIC * square))
-    lift = 0.5 * (1.0 + tangent)
-    slope = lift + 0.5 * values * (1.0 - tangent * tangent) * (COEF + (3.0 * COEF * CUBIC) * square)
-    return values * lift, slope
+    share = 0.5 + 0.5 * jnp.tanh(values * (COEF + (COEF * CUBIC) * square))
+    value = values * share
+    slope = share + value * (1.0 - share) * (2.0 * COEF + (6.0 * COEF * CUBIC) * square)
+    return value, slope
 
 
 CHUNK = 256
@@ -695,7 +695,8 @@
 def step_kernel(
     slides, cotangent, kernel, kernel_bias, norm_gain, norm_bias, bias_out, layer_scale, bias_in,
     shard_in, shard_out,
-    output, grad_slides, final_in, final_out, final_small,
+    output_end, grad_slides_end, final_in_end, final_out_end, final_small_end,
+    output, grad_slides, final_in, final_out, final_small, leave_sems,
     full_in, full_out, padded0, padded1, padded_g0, padded_g1, result, taps,
     normed, rstd, normal, turned, act, slope, hidden_grad, branch, carry, upstream, low,
     gm_tile, middle, grad_in, grad_out, small,
@@ -723,6 +724,13 @@
             ends = (grad_out.at[which], final_out.at[which])
         ways[kind, which] = Reduction(me, kind, early, *ends, bufs, sems)
 
+    leaving = []
+
+    def send_out(source, target):
+        copy = pltpu.make_async_copy(source, target, leave_sems.at[len(leaving)])
+        copy.start()
+        leaving.append(copy)
+
     little = SmallReduction(me, small, final_small, scratch[-4:-1], scratch[-1])
 
     def reducing(which):
@@ -833,15 +841,16 @@
         total = values[0:8] + values[8:16] + (values[16:24] + values[24:32])
         carry[which, slot] = carry[which, slot] + total
 
-    def weight_grads(which):
+    def weight_grads(which, first=0, last=2048 // CHUNK):
         def chunk(c, _):
             cols = part(c * CHUNK, CHUNK)
             grad_out[which, cols, :] = dot(act[which, :, cols], low[...], 0, 0).astype(BF)
             grad_in[which, :, cols] = dot(turned[...], hidden_grad[:, cols]).astype(BF)
             return 0
 
-        turned[...] = normal[which].T
-        lax.fori_loop(0, 2048 // CHUNK, chunk, 0)
+        if first == 0:
+            turned[...] = normal[which].T
+        lax.fori_loop(first, last, chunk, 0)
 
     def normal_grads(which, target):
         def chunk(n, _):
@@ -967,32 +976,38 @@
 
     with scope("p19_hidden0"):
         hidden_grads(0, slope, 2048 // CHUNK)
-    go("p20_go1", out1, in1)
     with scope("p21_wgrads0"):
-        weight_grads(0)
+        weight_grads(0, 0, 4)
+    go("p21_go1", out1, in1)
+    with scope("p21_wgrads0b"):
+        weight_grads(0, 4)
     in0.advance()
     out0.advance()
     with scope("p23_ngrads0"):
         normal_grads(0, normed.at[1])
-    go("p23_go1", out1, in1)
+    go("p23_go1", out1)
     go("p23_go0", in0)
     with scope("p24_leave0"):
         leave(0, normed.at[1])
         halos[3].start()
+    go("p25_go1", in1)
     go("p25_go0", out0)
     with scope("p26_contract1"):
         contract(1)
         residual(1, output)
+        send_out(output, output_end)
         scale_grad(1, from_cotangent)
         settle(1)
         settle(0)
-    go("p27_go1", in1, out1)
     with scope("p28_taps0"):
         tap_grads(padded0, padded_g0, small, 0, range(7))
     go("p29_go0", in0)
-    go("p29_go1", in1)
+    go("p29_go1", in1, out1)
     with scope("p29_taps1"):
-        tap_grads(padded1, padded_g1, small, 64, range(7))
+        tap_grads(padded1, padded_g1, small, 64, range(4))
+    go("p29b_go0", out0)
+    with scope("p29_taps1b"):
+        tap_grads(padded1, padded_g1, small, 64, range(4, 7))
     little.advance()
     go("p30_go0", in0)
     go("p30_go0b", out0)
@@ -1001,17 +1016,17 @@
         halos[3].finish()
     with scope("p31_depth0"):
         depthwise(padded_g0, taps.at[0], result, True, 0, 16)
-    go("p31_go", little, in0, out0)
+    go("p31_go", little, in0, out0, in1)
     with scope("p33_depth0"):
         depthwise(padded_g0, taps.at[0], result, True, 16, 32)
-    go("p33_go", in0, little, out0)
+    go("p33_go", in0, little, out0, out1)
     with scope("p33_depth0b"):
         for r in range(16):
             rows = slice(r * 32, r * 32 + 32)
             grad_slides[rows, :] = (upstream[rows, :] + pixels(result, r)).astype(BF)
-    go("p34_go", in0, little, out0, out1, in1)
+        send_out(grad_slides, grad_slides_end)
+    go("p34_go", in0, little, in1)
     go("p35_go", in0, little, out0)
-    go("p36_go", in0, little, out0, out1, in1)
     every = [out1, in1, little, out0, in0]
     with scope("p38_rest"):
         while any(way.steps for way in every):
@@ -1019,8 +1034,14 @@
                 if way.steps:
                     way.advance()
     with scope("p39_drain"):
+        for which in (1, 0):
+            send_out(final_in.at[which], final_in_end.at[which])
+            send_out(final_out.at[which], final_out_end.at[which])
+        send_out(final_small, final_small_end)
         for way in every + halos + [gather]:
             way.drain()
+        for copy in leaving:
+            copy.wait()
 
 
 def halo_scratch():
@@ -1038,6 +1059,12 @@
     vmem = pl.BlockSpec(memory_space=pltpu.VMEM)
     grid = pltpu.VMEM((BACK * SPAN * 8, 128), F32)
     scratch = [
+        pltpu.VMEM((512, 512), BF),
+        pltpu.VMEM((512, 512), BF),
+        pltpu.VMEM((2, 256, 2048), BF),
+        pltpu.VMEM((2, 2048, 256), BF),
+        pltpu.VMEM((128, 512), F32),
+        pltpu.SemaphoreType.DMA((7,)),
         pltpu.VMEM((2, 512, 2048), BF),
         pltpu.VMEM((2, 2048, 512), BF),
         grid,
@@ -1085,7 +1112,7 @@
             jax.ShapeDtypeStruct((128, 512), F32),
         ),
         in_specs=[vmem] * 9 + [pl.BlockSpec(memory_space=pl.ANY)] * 2,
-        out_specs=[vmem] * 5,
+        out_specs=[pl.BlockSpec(memory_space=pl.ANY)] * 5,
         scratch_shapes=scratch + extra + reductions,
         compiler_params=pltpu.CompilerParams(
             collective_id=0, has_side_effects=True, vmem_limit_bytes=67043328

time: 129 us -> 128 us (level)
  no operation moved by 1% of the time
where the time goes in v4:
time: 128 us
  Pallas kernels  127 us (99%)
    pallas_call x1, Pallas kernels, whole_step(): pl.pallas_call(step_kernel, out_shape=(jax.ShapeDtypeStruct((512, 512), B...  120 us
    pallas_call x1, Pallas kernels, unpack(): pl.pallas_call(unpack_kernel, out_shape=(jax.ShapeDtypeStruct((512, 512),...  6.63 us

profile of v4, /device:TPU:1, one launch (start us, length us, event | category | flops | bytes accessed | tf_op | source)
XLA Modules:
  0.0 127.8 jit_solution(9655612658418931783)
XLA Ops:
  0.6 120.4 %whole_step.1 = (bf16[512,512]{1,0:T(8,128)(2,1)}, bf16[512,512]{1,0:T(8,128)(2,1)}, bf16[2,256,2048]{2,1,0:T(8,128)(2,1)}, bf16[2,2048,256]{2,1,0:T(8,128)(2,1)}, f32[128,512]{1,0:T(8,128)}) custom-call(bf16[512,512]{1,0:T(8,128)(2,1)} %bitcast.7, bf16[512,512]{1,0:T(8,128)(2,1)} %bitcast.8, f32[7,7,2,512]{3,2,1,0:T(2,128)} %bitcast.9, ...), custom_call_target="tpu_custom_call" | custom-call | tf_op jit(solution)/shard_map/whole_step/pallas_call | solution.py:1105
  121.0 6.6 %unpack.1 = (bf16[512,512]{1,0:T(8,128)(2,1)}, bf16[512,512]{1,0:T(8,128)(2,1)}, f32[2,256,2048]{2,1,0:T(8,128)}, f32[2,2048,256]{2,1,0:T(8,128)}, f32[7,7,2,512...) custom-call(bf16[512,512]{1,0:T(8,128)(2,1)} %get-tuple-element.19.output, ...), custom_call_target="tpu_custom_call" | custom-call | tf_op jit(solution)/shard_map/unpack/pallas_call | solution.py:1162

commit v5 on v4

--- a/solution.py
+++ b/solution.py
@@ -841,16 +841,15 @@
         total = values[0:8] + values[8:16] + (values[16:24] + values[24:32])
         carry[which, slot] = carry[which, slot] + total
 
-    def weight_grads(which, first=0, last=2048 // CHUNK):
+    def weight_grads(which):
         def chunk(c, _):
             cols = part(c * CHUNK, CHUNK)
             grad_out[which, cols, :] = dot(act[which, :, cols], low[...], 0, 0).astype(BF)
             grad_in[which, :, cols] = dot(turned[...], hidden_grad[:, cols]).astype(BF)
             return 0
 
-        if first == 0:
-            turned[...] = normal[which].T
-        lax.fori_loop(first, last, chunk, 0)
+        turned[...] = normal[which].T
+        lax.fori_loop(0, 2048 // CHUNK, chunk, 0)
 
     def normal_grads(which, target):
         def chunk(n, _):
@@ -977,20 +976,16 @@
     with scope("p19_hidden0"):
         hidden_grads(0, slope, 2048 // CHUNK)
     with scope("p21_wgrads0"):
-        weight_grads(0, 0, 4)
-    go("p21_go1", out1, in1)
-    with scope("p21_wgrads0b"):
-        weight_grads(0, 4)
+        weight_grads(0)
     in0.advance()
     out0.advance()
+    go("p21_go1", out1, in1)
     with scope("p23_ngrads0"):
         normal_grads(0, normed.at[1])
-    go("p23_go1", out1)
     go("p23_go0", in0)
     with scope("p24_leave0"):
         leave(0, normed.at[1])
         halos[3].start()
-    go("p25_go1", in1)
     go("p25_go0", out0)
     with scope("p26_contract1"):
         contract(1)
@@ -999,34 +994,33 @@
         scale_grad(1, from_cotangent)
         settle(1)
         settle(0)
+    go("p27_go1", out1)
     with scope("p28_taps0"):
         tap_grads(padded0, padded_g0, small, 0, range(7))
     go("p29_go0", in0)
-    go("p29_go1", in1, out1)
+    go("p29_go1", in1)
     with scope("p29_taps1"):
-        tap_grads(padded1, padded_g1, small, 64, range(4))
-    go("p29b_go0", out0)
-    with scope("p29_taps1b"):
-        tap_grads(padded1, padded_g1, small, 64, range(4, 7))
+        tap_grads(padded1, padded_g1, small, 64, range(7))
     little.advance()
     go("p30_go0", in0)
     go("p30_go0b", out0)
-    go("p30_go1", out1, in1)
+    go("p30_go1", in1, out1)
     with scope("p30_halo3_end"):
         halos[3].finish()
     with scope("p31_depth0"):
         depthwise(padded_g0, taps.at[0], result, True, 0, 16)
-    go("p31_go", little, in0, out0, in1)
+    go("p31_go", little, in0, out0, in1, out1)
     with scope("p33_depth0"):
         depthwise(padded_g0, taps.at[0], result, True, 16, 32)
-    go("p33_go", in0, little, out0, out1)
+    go("p33_go", in0, little, out0, in1)
     with scope("p33_depth0b"):
         for r in range(16):
             rows = slice(r * 32, r * 32 + 32)
             grad_slides[rows, :] = (upstream[rows, :] + pixels(result, r)).astype(BF)
         send_out(grad_slides, grad_slides_end)
-    go("p34_go", in0, little, in1)
-    go("p35_go", in0, little, out0)
+    go("p34_go", in0, little, out0, out1)
+    go("p35_go", in0, little, out0, in1)
+    go("p36_go", in0, little, out0, out1, in1)
     every = [out1, in1, little, out0, in0]
     with scope("p38_rest"):
         while any(way.steps for way in every):

time: 128 us -> 126 us (0.984)
    pallas_call x1, Pallas kernels: 120 us -> 119 us  [whole_step(): pl.pallas_call(step_kernel, out_shape=(jax.ShapeDtypeStruct((512, 512), B...]
where the time goes in v5:
time: 126 us
  Pallas kernels  126 us (100%)
    pallas_call x1, Pallas kernels, whole_step(): pl.pallas_call(step_kernel, out_shape=(jax.ShapeDtypeStruct((512, 512), B...  119 us
    pallas_call x1, Pallas kernels, unpack(): pl.pallas_call(unpack_kernel, out_shape=(jax.ShapeDtypeStruct((512, 512),...  6.63 us

profile of v5, /device:TPU:1, one launch (start us, length us, event | category | flops | bytes accessed | tf_op | source)
XLA Modules:
  0.0 126.3 jit_solution(16654302397462416288)
XLA Ops:
  0.6 118.9 %whole_step.1 = (bf16[512,512]{1,0:T(8,128)(2,1)}, bf16[512,512]{1,0:T(8,128)(2,1)}, bf16[2,256,2048]{2,1,0:T(8,128)(2,1)}, bf16[2,2048,256]{2,1,0:T(8,128)(2,1)}, f32[128,512]{1,0:T(8,128)}) custom-call(bf16[512,512]{1,0:T(8,128)(2,1)} %bitcast.7, bf16[512,512]{1,0:T(8,128)(2,1)} %bitcast.8, f32[7,7,2,512]{3,2,1,0:T(2,128)} %bitcast.9, ...), custom_call_target="tpu_custom_call" | custom-call | tf_op jit(solution)/shard_map/whole_step/pallas_call | solution.py:1099
  119.5 6.6 %unpack.1 = (bf16[512,512]{1,0:T(8,128)(2,1)}, bf16[512,512]{1,0:T(8,128)(2,1)}, f32[2,256,2048]{2,1,0:T(8,128)}, f32[2,2048,256]{2,1,0:T(8,128)}, f32[7,7,2,512...) custom-call(bf16[512,512]{1,0:T(8,128)(2,1)} %get-tuple-element.19.output, ...), custom_call_target="tpu_custom_call" | custom-call | tf_op jit(solution)/shard_map/unpack/pallas_call | solution.py:1156
